TPU v7x, 8 devices: a whole 2x2x1 slice. The times are simulated.
8 devices in a mesh: sp: 8 (over z, y, x, core).
Axes of the slice: x: 2, y: 2, z: 1, core: 2. Of those that a mesh axis runs over, the one named last changes fastest.
Arguments:
- x: bfloat16 [4096, 1024], P('sp')
- seg_ids: int32 [4096], P('sp')
- positions: int32 [4096], P('sp')
- grad_y: bfloat16 [4096, 1024], P('sp')
- norm1_gain: bfloat16 [1024], P('sp')
- w_q: bfloat16 [1024, 16, 64], P('sp')
- w_k: bfloat16 [1024, 16, 64], P('sp')
- w_v: bfloat16 [1024, 16, 64], P('sp')
- w_o: bfloat16 [16, 64, 1024], P('sp')
- norm2_gain: bfloat16 [1024], P('sp')
- w_gate: bfloat16 [1024, 2816], P('sp')
- w_up: bfloat16 [1024, 2816], P('sp')
- w_down: bfloat16 [2816, 1024], P('sp')
Outputs:
- output 1: bfloat16 [4096, 1024], P('sp')
- output 2: bfloat16 [4096, 1024], P('sp')
- output 3: float32 [1024], P('sp')
- output 4: float32 [1024, 16, 64], P('sp')
- output 5: float32 [1024, 16, 64], P('sp')
- output 6: float32 [1024, 16, 64], P('sp')
- output 7: float32 [16, 64, 1024], P('sp')
- output 8: float32 [1024], P('sp')
- output 9: float32 [1024, 2816], P('sp')
- output 10: float32 [1024, 2816], P('sp')
- output 11: float32 [2816, 1024], P('sp')
All inputs are finite; a program needn't handle non-finite values.
Results may differ from a plain program's by a relative error of at most 0.0158321.
Values are sent between devices in bfloat16 or wider.
A program may use at most 1 GiB of HBM per device.

v0:
```python
import jax
import jax.numpy as jnp
from jax import lax
from jax.experimental import pallas as pl
from jax.experimental.pallas import tpu as pltpu
from jax.sharding import PartitionSpec as P


NORM_EPS = 1e-5
ROPE_BASE = 10000.0
SEQ = 4096
D = 1024
HD = 64
FF = 2816
NDEV = 8
TOK = SEQ // NDEV
LANES = 128
BQ = 256
BK = 512
NQ = SEQ // BQ
NEG = -1e30
F32 = jnp.float32
BF16 = jnp.bfloat16


def dot_nt(a, b):
    return lax.dot_general(a, b, (((1,), (1,)), ((), ())), preferred_element_type=F32)


def dot_tn(a, b):
    return lax.dot_general(a, b, (((0,), (0,)), ((), ())), preferred_element_type=F32)


def head_pair(t):
    lane = lax.broadcasted_iota(jnp.int32, (1, LANES), 1)
    low = (lane < HD).astype(F32).astype(BF16)
    high = (lane >= HD).astype(F32).astype(BF16)
    return jnp.concatenate([t * low, t * high], axis=0)


def rope_back_tile(t, cos_t, sin_t):
    lane = lax.broadcasted_iota(jnp.int32, t.shape, 1)
    first_half = lax.rem(lane, HD) < HD // 2
    rotated = jnp.where(first_half, -pltpu.roll(t, LANES - HD // 2, 1), pltpu.roll(t, HD // 2, 1))
    return t * cos_t - rotated * sin_t


def attn_fwd_kernel(lo_ref, start_ref, q_ref, k_ref, v_ref, o_ref, lse_ref, acc_ref):
    q_iota = lax.rem(lax.broadcasted_iota(jnp.int32, (1, 2 * BQ), 1), BQ)

    def q_block(i, _):
        q_start = pl.multiple_of(i * BQ, BQ)
        q2 = head_pair(q_ref[pl.ds(q_start, BQ), :])
        first = start_ref[pl.ds(i, 1), :]
        q_index = q_start + q_iota
        acc_ref[...] = jnp.zeros_like(acc_ref)

        def k_block(j, carry):
            m_old, l_old = carry
            k_start = pl.multiple_of(j * BK, BK)
            k = k_ref[pl.ds(k_start, BK), :]
            v = v_ref[pl.ds(k_start, BK), :]
            s = dot_nt(k, q2)
            k_index = k_start + lax.broadcasted_iota(jnp.int32, s.shape, 0)
            s = jnp.where((k_index >= first) & (k_index <= q_index), s, NEG)
            m_new = jnp.maximum(m_old, jnp.max(s, axis=0, keepdims=True))
            p = jnp.exp(s - m_new)
            alpha = jnp.exp(m_old - m_new)
            l_new = alpha * l_old + jnp.sum(p, axis=0, keepdims=True)
            acc_ref[...] = acc_ref[...] * alpha + dot_tn(v, p.astype(BF16))
            return m_new, l_new

        init = (jnp.full((1, 2 * BQ), NEG, F32), jnp.zeros((1, 2 * BQ), F32))
        m_fin, l_fin = lax.fori_loop(lax.div(lo_ref[i, 0], BK), (q_start + BQ - 1) // BK + 1, k_block, init)
        lse_ref[pl.ds(i, 1), :] = m_fin + jnp.log(l_fin)
        out = acc_ref[...] * (1.0 / l_fin)
        out = jnp.concatenate([out[:HD, :BQ], out[HD:, BQ:]], axis=0)
        o_ref[pl.ds(q_start, BQ), :] = out.T.astype(BF16)
        return 0

    lax.fori_loop(0, NQ, q_block, 0)


def attn_bwd_kernel(lo_ref, start_ref, lse_ref, q_ref, k_ref, v_ref, o_ref, do_ref, cos_ref, sin_ref,
                    out_ref, dk_acc, dv_acc, dq_acc):
    q_iota = lax.rem(lax.broadcasted_iota(jnp.int32, (1, 2 * BQ), 1), BQ)
    dk_acc[...] = jnp.zeros_like(dk_acc)
    dv_acc[...] = jnp.zeros_like(dv_acc)

    def q_block(i, _):
        q_start = pl.multiple_of(i * BQ, BQ)
        q2 = head_pair(q_ref[pl.ds(q_start, BQ), :])
        do = do_ref[pl.ds(q_start, BQ), :]
        do2 = head_pair(do)
        prod = (do.astype(F32) * o_ref[pl.ds(q_start, BQ), :].astype(F32)).T
        delta = jnp.concatenate([jnp.sum(prod[:HD], axis=0, keepdims=True),
                                 jnp.sum(prod[HD:], axis=0, keepdims=True)], axis=1)
        first = start_ref[pl.ds(i, 1), :]
        lse = lse_ref[pl.ds(i, 1), :]
        q_index = q_start + q_iota
        dq_acc[...] = jnp.zeros_like(dq_acc)

        def k_block(j, _):
            k_start = pl.multiple_of(j * BK, BK)
            k = k_ref[pl.ds(k_start, BK), :]
            v = v_ref[pl.ds(k_start, BK), :]
            s = dot_nt(k, q2)
            k_index = k_start + lax.broadcasted_iota(jnp.int32, s.shape, 0)
            s = jnp.where((k_index >= first) & (k_index <= q_index), s, NEG)
            p = jnp.exp(s - lse)
            dp = dot_nt(v, do2).astype(BF16).astype(F32)
            ds = (p * (dp - delta)).astype(BF16)
            dv_acc[pl.ds(k_start, BK), :] += jnp.dot(p.astype(BF16), do2, preferred_element_type=F32)
            dk_acc[pl.ds(k_start, BK), :] += jnp.dot(ds, q2, preferred_element_type=F32)
            dq_acc[...] += dot_tn(k, ds)
            return 0

        lax.fori_loop(lax.div(lo_ref[i, 0], BK), (q_start + BQ - 1) // BK + 1, k_block, 0)
        dq = jnp.concatenate([dq_acc[:HD, :BQ], dq_acc[HD:, BQ:]], axis=0).T * (HD ** -0.5)
        rows = pl.ds(q_start, BQ)
        dq = dq.astype(BF16).astype(F32)
        out_ref[rows, 0:LANES] = rope_back_tile(dq, cos_ref[rows, :], sin_ref[rows, :]).astype(BF16)
        return 0

    lax.fori_loop(0, NQ, q_block, 0)

    def finish(i, _):
        rows = pl.ds(pl.multiple_of(i * BQ, BQ), BQ)
        dk = dk_acc[rows, :].astype(BF16).astype(F32)
        out_ref[rows, LANES:2 * LANES] = rope_back_tile(dk, cos_ref[rows, :], sin_ref[rows, :]).astype(BF16)
        out_ref[rows, 2 * LANES:3 * LANES] = dv_acc[rows, :].astype(BF16)
        return 0

    lax.fori_loop(0, NQ, finish, 0)


VMEM_SPEC = pl.BlockSpec(memory_space=pltpu.VMEM)
SMEM_SPEC = pl.BlockSpec(memory_space=pltpu.SMEM)


def attn_forward(start, q, k, v):
    return pl.pallas_call(
        attn_fwd_kernel,
        out_shape=(jax.ShapeDtypeStruct((SEQ, LANES), BF16), jax.ShapeDtypeStruct((NQ, 2 * BQ), F32)),
        in_specs=[SMEM_SPEC] + [VMEM_SPEC] * 4,
        out_specs=(VMEM_SPEC, VMEM_SPEC),
        scratch_shapes=[pltpu.VMEM((LANES, 2 * BQ), F32)],
        compiler_params=pltpu.CompilerParams(vmem_limit_bytes=40 * 1024 * 1024),
        cost_estimate=pl.CostEstimate(flops=20_000_000_000, bytes_accessed=5_000_000, transcendentals=20_000_000),
        name='attn_fwd',
    )(start, start, q, k, v)


def attn_backward(start, lse, q, k, v, o, do, cos_t, sin_t):
    return pl.pallas_call(
        attn_bwd_kernel,
        out_shape=jax.ShapeDtypeStruct((SEQ, 3 * LANES), BF16),
        in_specs=[SMEM_SPEC] + [VMEM_SPEC] * 9,
        out_specs=VMEM_SPEC,
        scratch_shapes=[pltpu.VMEM((SEQ, LANES), F32), pltpu.VMEM((SEQ, LANES), F32),
                        pltpu.VMEM((LANES, 2 * BQ), F32)],
        compiler_params=pltpu.CompilerParams(vmem_limit_bytes=48 * 1024 * 1024),
        cost_estimate=pl.CostEstimate(flops=50_000_000_000, bytes_accessed=12_000_000, transcendentals=20_000_000),
        name='attn_bwd',
    )(start, start, lse, q, k, v, o, do, cos_t, sin_t)


def head_kernel(x_ref, w_ref, small_ref, freq_ref, wo_ref, u_hbm, q_ref, k_ref, v_ref, cos_ref, sin_ref, all_small,
                start_ref, wo_out, x_buf, w_buf, w_ext, u_buf, small_send, small_recv, w_send, w_recv, x_send, x_recv,
                wo_send, wo_recv, u_sem):
    me = lax.axis_index('sp')
    core = lax.rem(me, 2)
    x_pos = lax.rem(me // 2, 2)
    y_pos = me // 4
    step_c, step_x, step_y = 1 - 2 * core, 2 - 4 * x_pos, 4 - 8 * y_pos
    mate, near_x, near_y, diag = me + step_c, me + step_x, me + step_y, me + step_x + step_y

    barrier = pltpu.get_barrier_semaphore()
    for n in range(1, NDEV):
        pl.semaphore_signal(barrier, inc=1, device_id=(lax.rem(me + n, NDEV),), device_id_type=pl.DeviceIdType.MESH)
    pl.semaphore_wait(barrier, NDEV - 1)

    def remote(src, dst, send_sem, recv_sem, dev):
        return pltpu.make_async_remote_copy(src_ref=src, dst_ref=dst, send_sem=send_sem, recv_sem=recv_sem,
                                            device_id=(dev,), device_id_type=pl.DeviceIdType.MESH)

    def half(ref, h):
        rows = ref.shape[0] // 2
        return ref.at[pl.ds(h * rows, rows), :]

    def x_copy(slot, src_dev, h, target, from_ref=None):
        source = half(x_buf.at[src_dev], h) if from_ref is None else half(from_ref, h)
        return remote(source, half(x_buf.at[src_dev], h), x_send.at[slot], x_recv.at[slot], target)

    def wo_copy(slot, src_dev, h, target, from_ref=None):
        source = half(wo_out.at[src_dev], h) if from_ref is None else half(from_ref, h)
        return remote(source, half(wo_out.at[src_dev], h), wo_send.at[slot], wo_recv.at[slot], target)

    def first_sends(copy, from_ref):
        return [copy(0, me, 0, near_x, from_ref), copy(3, me, 1, near_y, from_ref),
                copy(1, me, 1, near_x, from_ref), copy(2, me, 0, near_y, from_ref),
                copy(12, me, 0, mate, from_ref), copy(13, me, 1, mate, from_ref)]

    smalls = [remote(small_ref, all_small.at[me], small_send.at[n - 1], small_recv.at[n - 1], lax.rem(me + n, NDEV))
              for n in range(1, NDEV)]
    weights = [remote(w_ref.at[lax.rem(me + n, NDEV)], w_buf.at[me], w_send.at[n - 1], w_recv.at[n - 1],
                      lax.rem(me + n, NDEV)) for n in range(1, NDEV)]
    for c in smalls:
        c.start()
    for c in weights:
        c.start()
    own = first_sends(x_copy, x_ref)
    for c in own:
        c.start()

    all_small[me] = small_ref[...]
    w_buf[me] = w_ref[me]
    for c in smalls + weights:
        c.wait_recv()

    lane = lax.broadcasted_iota(jnp.int32, (LANES, LANES), 1)
    first_half = lax.rem(lane, HD) < HD // 2

    def build(i, _):
        rows = pl.ds(pl.multiple_of(i * LANES, LANES), LANES)
        w_ext[rows, 0:3 * LANES] = w_buf[i]
        for n in range(2):
            t = w_buf[i, :, n * LANES:(n + 1) * LANES].astype(F32)
            rot = jnp.where(first_half, -pltpu.roll(t, LANES - HD // 2, 1), pltpu.roll(t, HD // 2, 1))
            w_ext[rows, (3 + n) * LANES:(4 + n) * LANES] = rot.astype(BF16)
        return 0

    lax.fori_loop(0, NDEV, build, 0)
    gain1 = jnp.concatenate([all_small[n, 0:1, :] for n in range(NDEV)], axis=1)

    def process(order, src_ref, src_dev, h):
        def part(i, _):
            local = pl.ds(pl.multiple_of(h * (TOK // 2) + i * LANES, LANES), LANES)
            rows = pl.ds(pl.multiple_of(src_dev * TOK + h * (TOK // 2) + i * LANES, LANES), LANES)
            xv = src_ref[local, :].astype(F32)
            inv = lax.rsqrt(jnp.mean(xv * xv, axis=-1, keepdims=True) + NORM_EPS)
            u = (xv * inv * gain1).astype(BF16)
            u_buf[rows, :] = u
            proj = jnp.dot(u, w_ext[...], preferred_element_type=F32)
            angle = freq_ref[...] * all_small[src_dev, pl.ds(2 + 2 * h + i, 1), :]
            cos4, sin4 = jnp.cos(angle), jnp.sin(angle)
            cos_v = jnp.concatenate([cos4] * 4, axis=0).T
            sin_v = jnp.concatenate([sin4] * 4, axis=0).T
            cos_ref[rows, :] = cos_v
            sin_ref[rows, :] = sin_v
            q = (proj[:, :LANES] * cos_v + proj[:, 3 * LANES:4 * LANES] * sin_v).astype(BF16).astype(F32)
            q_ref[rows, :] = (q * (HD ** -0.5)).astype(BF16)
            k_ref[rows, :] = (proj[:, LANES:2 * LANES] * cos_v + proj[:, 4 * LANES:] * sin_v).astype(BF16)
            v_ref[rows, :] = proj[:, 2 * LANES:3 * LANES].astype(BF16)
            return 0

        lax.fori_loop(0, 2, part, 0)
        u_rows = pl.ds(pl.multiple_of(src_dev * TOK + h * (TOK // 2), TOK // 2), TOK // 2)
        out = pltpu.make_async_copy(u_buf.at[u_rows, :], u_hbm.at[u_rows, :], u_sem.at[order])
        out.start()
        return out

    pending = []
    copies = list(own)

    def arrive(copy, slot, src_dev, h):
        copy(slot, src_dev, h, mate).wait_recv()

    def pass_on(copy, slot, src_dev, h, target):
        c = copy(slot, src_dev, h, target)
        c.start()
        copies.append(c)

    def relay(copy, slot, src_dev, h):
        arrive(copy, slot, src_dev, h)
        if slot == 0:
            pass_on(copy, 4, src_dev, h, near_y)
        elif slot == 3:
            pass_on(copy, 5, src_dev, h, near_x)
        pass_on(copy, 6 + slot, src_dev, h, mate)

    def work(src_ref, src_dev, h):
        pending.append(process(len(pending), src_ref, src_dev, h))

    work(x_ref, me, 0)
    work(x_ref, me, 1)
    arrivals = [(0, near_x, 0), (3, near_y, 1), (1, near_x, 1), (2, near_y, 0), (4, diag, 0), (5, diag, 1)]
    late = [(12, mate, 0), (13, mate, 1)]
    for n, (slot, src_dev, h) in enumerate(arrivals):
        relay(x_copy, slot, src_dev, h)
        if n == 1:
            wo_own = first_sends(wo_copy, wo_ref)
            for c in wo_own:
                c.start()
            copies += wo_own
            wo_out[me] = wo_ref[...]
        if n >= 4:
            relay(wo_copy, *arrivals[n - 4])
        work(x_buf.at[src_dev], src_dev, h)
        mate_slot, mate_src, mate_h = late.pop(0)
        arrive(x_copy, mate_slot, mate_src, mate_h)
        work(x_buf.at[mate_src], mate_src, mate_h)
        late.append((6 + slot, src_dev + step_c, h))
    for n, (slot, src_dev, h) in enumerate(late):
        if n < 2:
            relay(wo_copy, *arrivals[n + 2])
        arrive(x_copy, slot, src_dev, h)
        work(x_buf.at[src_dev], src_dev, h)
    for n in range(NDEV):
        for h in range(2):
            row = jnp.concatenate([all_small[n, 2 + 2 * h:3 + 2 * h, :], all_small[n, 3 + 2 * h:4 + 2 * h, :]], axis=1)
            index = n * TOK + h * BQ + lax.broadcasted_iota(jnp.int32, (1, BQ), 1)
            first = index - row.astype(jnp.int32)
            start_ref[2 * n + h:2 * n + h + 1, :] = jnp.concatenate([first, first], axis=1)
    relay(wo_copy, *arrivals[4])
    relay(wo_copy, *arrivals[5])
    for slot, src_dev, h in [(12, mate, 0), (13, mate, 1)] + [(6 + m, d + step_c, h) for m, d, h in arrivals]:
        arrive(wo_copy, slot, src_dev, h)
    for c in pending:
        c.wait()
    for c in smalls + weights + copies:
        c.wait_send()


def head_stage(x, w_pieces, small, freq, w_o):
    dma = pltpu.SemaphoreType.DMA
    return pl.pallas_call(
        head_kernel,
        out_shape=(jax.ShapeDtypeStruct((SEQ, D), BF16),) + tuple(jax.ShapeDtypeStruct((SEQ, LANES), BF16) for _ in range(3))
        + tuple(jax.ShapeDtypeStruct((SEQ, LANES), F32) for _ in range(2))
        + (jax.ShapeDtypeStruct((NDEV, 8, LANES), F32), jax.ShapeDtypeStruct((NQ, 2 * BQ), jnp.int32),
           jax.ShapeDtypeStruct((NDEV, LANES, D), BF16)),
        in_specs=[VMEM_SPEC] * 5,
        out_specs=(pl.BlockSpec(memory_space=pl.ANY),) + (VMEM_SPEC,) * 8,
        scratch_shapes=[pltpu.VMEM((NDEV, TOK, D), BF16), pltpu.VMEM((NDEV, LANES, 3 * LANES), BF16),
                        pltpu.VMEM((D, 5 * LANES), BF16), pltpu.VMEM((SEQ, D), BF16),
                        dma((NDEV - 1,)), dma((NDEV - 1,)), dma((NDEV - 1,)), dma((NDEV - 1,)),
                        dma((14,)), dma((14,)), dma((14,)), dma((14,)), dma((16,))],
        compiler_params=pltpu.CompilerParams(collective_id=0, has_side_effects=True,
                                             vmem_limit_bytes=48 * 1024 * 1024),
        cost_estimate=pl.CostEstimate(flops=40_000_000_000, bytes_accessed=30_000_000, transcendentals=1_000_000),
        name='head_stage',
    )(x, w_pieces, small, freq, w_o)


COLS = D // 2
DN_ROWS = FF // NDEV
OUT_ROWS = DN_ROWS + LANES


def tail_kernel(mt_ref, gy_ref, ot_ref, gh_ref, d_ref, x_ref, h_ref, gz_ref, gain_ref, u_hbm, win_hbm,
                dn_out, wo_out, gw_out, gx_out, gain_out,
                mt_mate, gy_mate, ot_mate, gh_mate, part, box, d_buf, win_buf, u_buf, gw_mine, gain_mine, gain_buf,
                mate_send, mate_recv, rs_send, rs_recv, d_send, d_recv, gw_send, gw_recv, gg_send, gg_recv, win_sem, u_sem):
    me = lax.axis_index('sp')
    core = lax.rem(me, 2)
    x_pos = lax.rem(me // 2, 2)
    y_pos = me // 4
    step_c, step_x, step_y = 1 - 2 * core, 2 - 4 * x_pos, 4 - 8 * y_pos
    mate, near_x, near_y, diag = me + step_c, me + step_x, me + step_y, me + step_x + step_y

    win_copy = pltpu.make_async_copy(win_hbm, win_buf, win_sem)
    win_copy.start()
    u_copy = pltpu.make_async_copy(u_hbm, u_buf, u_sem)
    u_copy.start()

    barrier = pltpu.get_barrier_semaphore()
    for n in range(1, NDEV):
        pl.semaphore_signal(barrier, inc=1, device_id=(lax.rem(me + n, NDEV),), device_id_type=pl.DeviceIdType.MESH)
    pl.semaphore_wait(barrier, NDEV - 1)

    def remote(src, dst, send_sem, recv_sem, dev):
        return pltpu.make_async_remote_copy(src_ref=src, dst_ref=dst, send_sem=send_sem, recv_sem=recv_sem,
                                            device_id=(dev,), device_id_type=pl.DeviceIdType.MESH)

    def to_peers(src, dst, send_sem, recv_sem):
        return [remote(src.at[lax.rem(me + n, NDEV)], dst.at[me], send_sem.at[n - 1], recv_sem.at[n - 1],
                       lax.rem(me + n, NDEV)) for n in range(1, NDEV)]

    def dn_rows(dev):
        return pl.ds(pl.multiple_of(dev * DN_ROWS, 32), DN_ROWS)

    def wo_rows(dev):
        return pl.ds(pl.multiple_of(dev * LANES, LANES), LANES)

    swaps = []
    for q in range(NDEV // 2):
        dest = 2 * q + 1 - core
        swaps.append(remote(mt_ref.at[dn_rows(dest), :], mt_mate.at[q], mate_send.at[q], mate_recv.at[q], mate))
        swaps.append(remote(ot_ref.at[wo_rows(dest), :], ot_mate.at[q], mate_send.at[4 + q], mate_recv.at[4 + q], mate))
    swaps.append(remote(gy_ref, gy_mate, mate_send.at[8], mate_recv.at[8], mate))
    swaps.append(remote(gh_ref, gh_mate, mate_send.at[9], mate_recv.at[9], mate))
    for c in swaps:
        c.start()
    d_moves = to_peers(d_ref, d_buf, d_send, d_recv)
    gw_moves = to_peers(gw_mine, gw_out, gw_send, gw_recv)
    gg_moves = to_peers(gain_mine, gain_buf, gg_send, gg_recv)
    for c in d_moves:
        c.start()
    d_buf[me] = d_ref[me]
    for c in swaps:
        c.wait_recv()

    def compute(rel, dev, col):
        chip = dev // 2
        cols = pl.ds(col * COLS, COLS)
        part[rel, col, 0:DN_ROWS, :] = (
            jnp.dot(mt_ref[dn_rows(dev), :], gy_ref[:, cols], preferred_element_type=F32)
            + jnp.dot(mt_mate[chip], gy_mate[:, cols], preferred_element_type=F32))
        part[rel, col, DN_ROWS:OUT_ROWS, :] = (
            jnp.dot(ot_ref[wo_rows(dev), :], gh_ref[:, cols], preferred_element_type=F32)
            + jnp.dot(ot_mate[chip], gh_mate[:, cols], preferred_element_type=F32))

    moves = [remote(part.at[3, 0], box.at[0], rs_send.at[0], rs_recv.at[0], near_x),
             remote(part.at[3, 1], box.at[1], rs_send.at[1], rs_recv.at[1], near_y),
             remote(part.at[1, 0], box.at[2], rs_send.at[2], rs_recv.at[2], near_x),
             remote(part.at[2, 1], box.at[3], rs_send.at[3], rs_recv.at[3], near_y),
             remote(part.at[2, 0], box.at[4], rs_send.at[4], rs_recv.at[4], near_y),
             remote(part.at[1, 1], box.at[5], rs_send.at[5], rs_recv.at[5], near_x)]
    compute(3, diag, 0)
    moves[0].start()
    compute(3, diag, 1)
    moves[1].start()
    compute(1, near_x, 0)
    moves[2].start()
    compute(2, near_y, 1)
    moves[3].start()
    compute(2, near_y, 0)
    compute(1, near_x, 1)
    u_copy.wait()

    def grad_win_piece(n, _):
        cols = pl.ds(pl.multiple_of(n * LANES, LANES), LANES)
        total = dot_tn(u_buf[0:TOK, cols], d_ref[0])
        for g in range(1, NDEV):
            total = total + dot_tn(u_buf[g * TOK:(g + 1) * TOK, cols], d_ref[g])
        gw_mine[n] = total
        return 0

    lax.fori_loop(0, NDEV, grad_win_piece, 0)
    for c in gw_moves:
        c.start()
    gw_out[me] = gw_mine[me]
    compute(0, me, 0)
    compute(0, me, 1)

    def add_box(rel, col, n):
        def rows_add(i, _):
            rows = pl.ds(pl.multiple_of(i * 32, 32), 32)
            part[rel, col, rows, :] += box[n, rows, :]
            return 0

        lax.fori_loop(0, OUT_ROWS // 32, rows_add, 0)

    moves[0].wait_recv()
    add_box(2, 0, 0)
    moves[4].start()
    moves[1].wait_recv()
    add_box(1, 1, 1)
    moves[5].start()

    for c in d_moves:
        c.wait_recv()
    win_copy.wait()
    gain1 = gain_ref[...]

    def grad_rows(i, carry):
        acc, acc2 = carry
        rows = pl.ds(pl.multiple_of(i * LANES, LANES), LANES)
        gu = dot_nt(d_buf[0, rows, :], win_buf[:, 0:3 * LANES])
        for g in range(1, NDEV):
            gu = gu + dot_nt(d_buf[g, rows, :], win_buf[:, g * 3 * LANES:(g + 1) * 3 * LANES])
        gu = gu.astype(BF16).astype(F32)
        xv = x_ref[rows, :].astype(F32)
        inv = lax.rsqrt(jnp.mean(xv * xv, axis=-1, keepdims=True) + NORM_EPS)
        normed = xv * inv
        acc = acc + jnp.sum(gu * normed, axis=0, keepdims=True)
        scaled = gu * gain1
        mean_term = jnp.mean(scaled * normed, axis=-1, keepdims=True)
        gx_out[rows, :] = (gh_ref[rows, :].astype(F32) + inv * (scaled - normed * mean_term)).astype(BF16)
        hv = h_ref[rows, :].astype(F32)
        normed2 = hv * lax.rsqrt(jnp.mean(hv * hv, axis=-1, keepdims=True) + NORM_EPS)
        acc2 = acc2 + jnp.sum(gz_ref[rows, :].astype(F32) * normed2, axis=0, keepdims=True)
        return acc, acc2

    gg1, gg2 = lax.fori_loop(0, TOK // LANES, grad_rows, (jnp.zeros((1, D), F32), jnp.zeros((1, D), F32)))
    for n in range(NDEV):
        piece = slice(n * LANES, (n + 1) * LANES)
        gain_mine[n] = jnp.concatenate([gg1[:, piece], gg2[:, piece], jnp.zeros((6, LANES), F32)], axis=0)
    for c in gg_moves:
        c.start()
    gain_buf[me] = gain_mine[me]

    moves[2].wait_recv()
    add_box(0, 0, 2)
    moves[3].wait_recv()
    add_box(0, 1, 3)
    for c in gg_moves:
        c.wait_recv()
    total = gain_buf[0]
    for n in range(1, NDEV):
        total = total + gain_buf[n]
    gain_out[...] = total
    for col in range(2):
        moves[4 + col].wait_recv()

        def finish(i, _):
            rows = pl.ds(pl.multiple_of(i * 32, 32), 32)
            dn_out[rows, col * COLS:(col + 1) * COLS] = part[0, col, rows, :] + box[4 + col, rows, :]
            return 0

        lax.fori_loop(0, DN_ROWS // 32, finish, 0)
        wo_out[:, col * COLS:(col + 1) * COLS] = part[0, col, DN_ROWS:OUT_ROWS, :] + box[4 + col, DN_ROWS:OUT_ROWS, :]
    for c in gw_moves:
        c.wait_recv()
    for c in swaps + d_moves + gw_moves + gg_moves + moves:
        c.wait_send()


def tail_stage(m_t, grad_y, o_t, grad_h, d_qkv, x, h_res, grad_z, gain1, u_all, win_full):
    dma = pltpu.SemaphoreType.DMA
    peers = (NDEV - 1,)
    return pl.pallas_call(
        tail_kernel,
        out_shape=(jax.ShapeDtypeStruct((DN_ROWS, D), F32), jax.ShapeDtypeStruct((LANES, D), F32),
                   jax.ShapeDtypeStruct((NDEV, LANES, 3 * LANES), F32), jax.ShapeDtypeStruct((TOK, D), BF16),
                   jax.ShapeDtypeStruct((8, LANES), F32)),
        in_specs=[VMEM_SPEC] * 9 + [pl.BlockSpec(memory_space=pl.ANY)] * 2,
        out_specs=(VMEM_SPEC,) * 5,
        scratch_shapes=[pltpu.VMEM((4, DN_ROWS, TOK), BF16), pltpu.VMEM((TOK, D), BF16),
                        pltpu.VMEM((4, LANES, TOK), BF16), pltpu.VMEM((TOK, D), BF16),
                        pltpu.VMEM((4, 2, OUT_ROWS, COLS), F32), pltpu.VMEM((6, OUT_ROWS, COLS), F32),
                        pltpu.VMEM((NDEV, TOK, 3 * LANES), BF16), pltpu.VMEM((D, 3 * D), BF16),
                        pltpu.VMEM((SEQ, D), BF16), pltpu.VMEM((NDEV, LANES, 3 * LANES), F32),
                        pltpu.VMEM((NDEV, 8, LANES), F32), pltpu.VMEM((NDEV, 8, LANES), F32),
                        dma((10,)), dma((10,)), dma((6,)), dma((6,)), dma(peers), dma(peers),
                        dma(peers), dma(peers), dma(peers), dma(peers), dma, dma],
        compiler_params=pltpu.CompilerParams(collective_id=1, has_side_effects=True,
                                             vmem_limit_bytes=60 * 1024 * 1024),
        cost_estimate=pl.CostEstimate(flops=60_000_000_000, bytes_accessed=60_000_000, transcendentals=1_000),
        name='tail_stage',
    )(m_t, grad_y, o_t, grad_h, d_qkv, x, h_res, grad_z, gain1, u_all, win_full)


def rms_back(grad_out, normed, inv_rms):
    mean_term = jnp.mean(grad_out * normed, axis=-1, keepdims=True)
    return inv_rms * (grad_out - normed * mean_term)


def solution(mesh):
    row_spec = P('sp', None)
    cube_spec = P('sp', None, None)
    vec_spec = P('sp')

    def gather(t):
        return lax.all_gather(t, 'sp', axis=0, tiled=True)

    def scatter_sum(t):
        return lax.psum_scatter(t, 'sp', scatter_dimension=0, tiled=True)

    def exchange(t):
        return lax.all_to_all(t, 'sp', 0, 0)

    def local_layer(x, seg_ids, positions, grad_y, norm1_gain, w_q, w_k, w_v, w_o, norm2_gain, w_gate, w_up, w_down):
        half = HD // 2
        inv_freq = (ROPE_BASE ** (-jnp.arange(half, dtype=F32) * 2.0 / HD))[:, None]
        freq = jnp.broadcast_to(inv_freq, (half, LANES))
        small = jnp.concatenate([norm1_gain.astype(F32)[None, :], norm2_gain.astype(F32)[None, :],
                                 positions.astype(F32).reshape(4, LANES), jnp.zeros((2, LANES), F32)])
        w_in = jnp.concatenate([t.reshape(LANES, NDEV, LANES) for t in (w_q, w_k, w_v)], axis=2)
        u_all, q, k, v, cos_t, sin_t, small, start2, wo_full = head_stage(
            x, w_in.transpose(1, 0, 2), small, freq, w_o.reshape(LANES, D))
        wo_full = wo_full.reshape(D, D)
        gain1 = small[:, 0].reshape(1, D)
        gain2 = small[:, 1].reshape(D)
        o_own, lse = attn_forward(start2, q, k, v)
        o_heads = exchange(o_own.reshape(NDEV, TOK, LANES))
        o_loc = o_heads.transpose(1, 0, 2).reshape(TOK, D)
        o_t = o_heads.transpose(0, 2, 1).reshape(D, TOK)

        wd_full = gather(w_down)
        wgu_full = gather(jnp.concatenate([w_gate, w_up], axis=1))
        win_full = gather(w_in.reshape(LANES, 3 * D))

        x_wide = x.astype(F32)
        h_res = (x_wide + jnp.dot(o_loc, wo_full, preferred_element_type=F32)).astype(BF16)
        h_wide = h_res.astype(F32)
        inv_rms2 = lax.rsqrt(jnp.mean(h_wide * h_wide, axis=-1, keepdims=True) + NORM_EPS)
        normed2 = h_wide * inv_rms2
        z_norm = (normed2 * gain2).astype(BF16)
        gate_up = jnp.dot(z_norm, wgu_full, preferred_element_type=F32)
        gate_pre, up_pre = gate_up[:, :FF], gate_up[:, FF:]
        gate_sig = jax.nn.sigmoid(gate_pre)
        gate_act = gate_pre * gate_sig
        mlp_act = (gate_act * up_pre).astype(BF16)

        grad_act = dot_nt(grad_y, wd_full).astype(BF16).astype(F32)
        grad_gate = (grad_act * up_pre * gate_sig * (1.0 + gate_pre * (1.0 - gate_sig))).astype(BF16)
        grad_up = (grad_act * gate_act).astype(BF16)
        grad_gu = jnp.concatenate([grad_gate, grad_up], axis=1)
        grad_wgu = scatter_sum(dot_tn(z_norm, grad_gu))
        grad_z_b = lax.optimization_barrier(dot_nt(grad_gu, wgu_full).astype(BF16))
        grad_z = grad_z_b.astype(F32)
        grad_h = (grad_y.astype(F32) + rms_back(grad_z * gain2, normed2, inv_rms2)).astype(BF16)
        grad_o = dot_nt(grad_h, wo_full).astype(BF16)
        grad_o = exchange(grad_o.reshape(TOK, NDEV, LANES).transpose(1, 0, 2)).reshape(SEQ, LANES)
        y = (h_wide + jnp.dot(mlp_act, wd_full, preferred_element_type=F32)).astype(BF16)

        d_qkv = attn_backward(start2, lse, q, k, v, o_own, grad_o, cos_t, sin_t)
        grad_wdown, grad_wo, grad_win, grad_x, grad_gains = tail_stage(
            mlp_act.T, grad_y, o_t, grad_h, d_qkv.reshape(NDEV, TOK, 3 * LANES), x, h_res, grad_z_b,
            gain1, u_all, win_full)
        grad_q, grad_k, grad_v = (grad_win[:, :, n * LANES:(n + 1) * LANES].transpose(1, 0, 2).reshape(LANES, 16, HD)
                                  for n in range(3))
        return (y, grad_x, grad_gains[0], grad_q, grad_k, grad_v, grad_wo.reshape(2, HD, D),
                grad_gains[1], grad_wgu[:, :FF], grad_wgu[:, FF:], grad_wdown)

    return jax.shard_map(
        local_layer, mesh=mesh,
        in_specs=(row_spec, vec_spec, vec_spec, row_spec, vec_spec, cube_spec, cube_spec, cube_spec, cube_spec,
                  vec_spec, row_spec, row_spec, row_spec),
        out_specs=(row_spec, row_spec, vec_spec, cube_spec, cube_spec, cube_spec, cube_spec, vec_spec,
                   row_spec, row_spec, row_spec),
        check_vma=False)
```

profile of v0, /device:TPU:0, one launch (start us, length us, event | category | flops | bytes accessed | tf_op | source)
XLA Modules:
  0.0 480.6 jit_solution(9273131632772663061)
XLA Ops:
  7.3 2.6 pad_maximum_fusion.5
  11.5 1.0 copy.44
  12.8 100.6 %head_stage.1 = (bf16[4096,1024]{1,0:T(8,128)(2,1)}, bf16[4096,128]{1,0:T(8,128)(2,1)S(1)}, bf16[4096,128]{1,0:T(8,128)(2,1)S(1)}, bf16[4096,128]{1,0:T(8,128)(2...) custom-call(bf16[512,1024]{1,0:T(8,128)(2,1)S(1)} %copy-done, ...), custom_call_target="tpu_custom_call" | custom-call | flops 40000000000 | bytes 30000000 | tf_op jit(solution)/shard_map/head_stage/pallas_call | solution.py:327
  113.5 31.4 %attn_fwd.1 = (bf16[4096,128]{1,0:T(8,128)(2,1)}, f32[16,512]{1,0:T(8,128)S(1)}) custom-call(s32[16,512]{1,0:T(8,128)S(1)} %get-tuple-element.27.lo_ref.start_ref, s32[16,512]{1,0:T(8,128)S(1)} %get-tuple-element.27.lo_ref.start_ref, bf16[4096,128]{1,0:T(8,128)(2,1)S(1)} %get-tuple-element.28.q_ref, bf16[4096,128]{1,0:T(8,128)(2,1)S(1)} %get-tuple-element.29.k_ref, ...), custom_call_target="tpu_custom_call" | custom-call | flops 20000000000 | bytes 5000000 | tf_op jit(solution)/shard_map/attn_fwd/pallas_call | solution.py:142
  144.8 3.0 all-to-all-start
  148.6 19.4 %all-to-all-done = bf16[8,512,128]{2,1,0:T(8,128)(2,1)} async-done(((bf16[8,512,128]{2,1,0:T(8,128)(2,1)}), bf16[8,512,128]{2,1,0:T(8,128)(2,1)}, u32[]{:S(2)}, u32[]{:S(2)}) %all-to-all-start) | async-done | bytes 1048608 | tf_op jit(solution)/shard_map/all_to_all | solution.py:562
  168.1 3.3 fusion.16
  171.4 12.3 %fusion.25 = f32[512,5632]{0,1:T(8,128)} fusion(bf16[1024,5632]{1,0:T(8,128)(2,1)} %all-gather.4.cloned.1.call-done, bf16[512,1024]{1,0:T(8,128)(2,1)S(1)} %get-tuple-element.58.h_ref, f32[1024]{0:T(1024)S(1)} %bitcast.78, f32[512]{0:T(512)S(1)} %add_rsqrt_fusion), kind=kOutput, calls=%fused_computation.42 | convolution fusion | flops 5907677184 | bytes 24123392 | tf_op jit(solution)/shard_map/dot_general | solution.py:591
  183.8 10.9 %fusion.2 = (bf16[512,2816]{0,1:T(8,128)(2,1)S(1)}, bf16[512,2816]{0,1:T(8,128)(2,1)S(1)}, bf16[512,2816]{0,1:T(8,128)(2,1)}) fusion(f32[512,5632]{0,1:T(8,128)} %fusion.25, bf16[512,1024]{1,0:T(8,128)(2,1)S(1)} %copy-done.10, bf16[2816,1024]{1,0:T(8,128)(2,1)} %all-gather.6.cloned.1.call-done), kind=kOutput, calls=%fused_computation.4 | convolution fusion | flops 2977300480 | bytes 27000832 | tf_op jit(solution)/shard_map/dot_general | solution.py:27
  194.7 1.6 copy-done.21
  196.2 1.1 copy-done.22
  197.3 13.6 %fusion.5 = f32[1024,5632]{1,0:T(8,128)} fusion(bf16[512,2816]{0,1:T(8,128)(2,1)S(1)} %get-tuple-element.44, bf16[512,2816]{0,1:T(8,128)(2,1)S(1)} %get-tuple-element.43, bf16[512,1024]{1,0:T(8,128)(2,1)S(1)} %get-tuple-element.58.h_ref, f32[1024]{0:T(1024)S(1)} %bitcast.79, f32[512]{0:T(512)S(1)} %add_rsqrt_fusion), kind=kOutput, calls=%fused_computation.11 | convolution fusion | flops 5919211520 | bytes 29890560 | tf_op jit(solution)/shard_map/dot_general | solution.py:31
  210.9 11.0 %fusion.19.gz_ref = bf16[512,1024]{1,0:T(8,128)(2,1)S(1)} fusion(bf16[1024,5632]{1,0:T(8,128)(2,1)} %all-gather.4.cloned.1.call-done, bf16[512,2816]{0,1:T(8,128)(2,1)} %copy-done.22, bf16[512,2816]{0,1:T(8,128)(2,1)} %copy-done.21), kind=kOutput, calls=%fused_computation.30 | convolution fusion | flops 5917638656 | bytes 18350080 | tf_op jit(solution)/shard_map/dot_general | solution.py:27
  223.3 1.5 copy-done.20
  224.8 1.3 fusion.20
  226.1 1.2 copy.46
  227.2 2.4 all-to-all-start.1
  229.6 2.4 copy.34
  231.9 10.2 %fusion.17 = bf16[512,1024]{1,0:T(8,128)(2,1)} fusion(bf16[512,1024]{1,0:T(8,128)(2,1)} %copy-done.6, bf16[512,2816]{0,1:T(8,128)(2,1)} %get-tuple-element.45, bf16[2816,1024]{1,0:T(8,128)(2,1)} %all-gather.6.cloned.1.call-done), kind=kOutput, calls=%fused_computation.26 | convolution fusion | flops 2954362880 | bytes 10747904 | tf_op jit(solution)/shard_map/dot_general | solution.py:607
  242.1 2.8 all-to-all-done.1
  244.9 1.2 copy-done.5
  246.1 47.2 %attn_bwd.1 = bf16[4096,384]{1,0:T(8,128)(2,1)} custom-call(s32[16,512]{1,0:T(8,128)S(1)} %get-tuple-element.27.lo_ref.start_ref, s32[16,512]{1,0:T(8,128)S(1)} %get-tuple-element.27.lo_ref.start_ref, f32[16,512]{1,0:T(8,128)S(1)} %get-tuple-element.34.lse_ref, bf16[4096,128]{1,0:T(8,128)(2,1)S(1)} %get-tuple-element.28.q_ref, ...), custom_call_target="tpu_custom_call" | custom-call | flops 49999998976 | bytes 12000000 | tf_op jit(solution)/shard_map/attn_bwd/pallas_call | solution.py:155
  293.3 168.1 %tail_stage.1 = (f32[352,1024]{1,0:T(8,128)}, f32[128,1024]{1,0:T(8,128)}, f32[8,128,384]{2,1,0:T(8,128)}, bf16[512,1024]{1,0:T(8,128)(2,1)}, f32[8,128]{1,0:T(8,128)}) custom-call(bf16[2816,512]{1,0:T(8,128)(2,1)} %bitcast.83, bf16[512,1024]{1,0:T(8,128)(2,1)} %gy_ref.1, bf16[1024,512]{1,0:T(8,128)(2,1)} %bitcast.70, bf16[512,1024]{1,0:T(8,128)(2,1)} %copy-done.12, ...), custom_call_target="tpu_custom_call" | custom-call | flops 60000002048 | bytes 60000000 | tf_op jit(solution)/shard_map/tail_stage/pallas_call | solution.py:523
  461.4 1.5 slice_bitcast_fusion
  462.9 1.0 copy.38
  463.9 1.0 copy.39
  464.9 1.0 copy.40
  465.9 1.3 slice_bitcast_fusion.4
  467.2 3.7 fusion.29
  470.8 1.0 copy.50
  471.8 0.8 copy.51
  472.6 1.1 copy.52
  (70 shorter events, 4.0 us)
Async XLA Ops:
  7.2 3.5 copy-start.14
  7.2 3.7 copy-start.15
  7.2 3.9 copy-start.16
  7.2 164.2 %all-gather.4.cloned.1.call-start = ((), (), s32[]{:S(2)}) async-start(), calls=%async_computation.3 | async-start | bytes 12976128 | tf_op jit(solution)/shard_map/all_gather | solution.py:556
  9.9 173.9 %all-gather.6.cloned.1.call-start = ((), (), s32[]{:S(2)}) async-start(), calls=%async_computation.4 | async-start | bytes 6488064 | tf_op jit(solution)/shard_map/all_gather | solution.py:556
  10.6 282.7 %all-gather.8.cloned.1.call-start = ((), (), s32[]{:S(2)}) async-start(), calls=%async_computation.5 | async-start | bytes 7077888 | tf_op jit(solution)/shard_map/all_gather | solution.py:556
  10.9 1.7 copy-start.17
  10.9 1.7 copy-start.18
  10.9 1.7 copy-start.19
  10.9 1.9 copy-start
  10.9 1.9 copy-start.1
  113.4 31.4 %copy-start.2 = (bf16[4096,128]{1,0:T(8,128)(2,1)}, bf16[4096,128]{1,0:T(8,128)(2,1)S(1)}, u32[]{:S(2)}) copy-start(bf16[4096,128]{1,0:T(8,128)(2,1)S(1)} %get-tuple-element.29.k_ref) | copy-start | bytes 3145732
  113.4 31.4 %copy-start.4 = (bf16[4096,128]{1,0:T(8,128)(2,1)}, bf16[4096,128]{1,0:T(8,128)(2,1)S(1)}, u32[]{:S(2)}) copy-start(bf16[4096,128]{1,0:T(8,128)(2,1)S(1)} %get-tuple-element.30.v_ref) | copy-start | bytes 3145732
  144.8 23.2 %all-to-all-start = ((bf16[8,512,128]{2,1,0:T(8,128)(2,1)}), bf16[8,512,128]{2,1,0:T(8,128)(2,1)}, u32[]{:S(2)}, u32[]{:S(2)}) async-start(bf16[8,512,128]{2,1,0:T(8,128)(2,1)} %bitcast.8), calls=%async_computation | async-start | bytes 2097152 | tf_op jit(solution)/shard_map/all_to_all | solution.py:562
  147.8 319.4 %reduce-scatter.2.cloned.1.call-start = ((), (), s32[]{:S(2)}) async-start(), calls=%async_computation.6 | async-start | bytes 25952256 | tf_op jit(solution)/shard_map/reduce_scatter | solution.py:559
  171.4 51.2 %copy-start.6 = (bf16[512,1024]{1,0:T(8,128)(2,1)}, bf16[512,1024]{1,0:T(8,128)(2,1)S(1)}, u32[]{:S(2)}) copy-start(bf16[512,1024]{1,0:T(8,128)(2,1)S(1)} %get-tuple-element.58.h_ref) | copy-start | bytes 3145732
  171.4 12.3 %copy-start.10 = (bf16[512,1024]{1,0:T(8,128)(2,1)S(1)}, bf16[512,1024]{1,0:T(8,128)(2,1)}, u32[]{:S(2)}) copy-start(bf16[512,1024]{1,0:T(8,128)(2,1)} %gy_ref.1) | copy-start | bytes 3145732
  194.7 1.6 copy-start.21
  194.7 2.6 copy-start.22
  210.9 11.6 %copy-start.11 = (bf16[512,1024]{1,0:T(8,128)(2,1)S(1)}, bf16[512,1024]{1,0:T(8,128)(2,1)}, u32[]{:S(2)}) copy-start(bf16[512,1024]{1,0:T(8,128)(2,1)} %gy_ref.1) | copy-start | bytes 3145732
  222.0 1.3 copy-start.7
  222.0 2.8 copy-start.20
  223.3 2.8 copy-start.12
  227.2 17.7 %all-to-all-start.1 = ((bf16[8,512,128]{2,1,0:T(8,128)(2,1)}), bf16[8,512,128]{2,1,0:T(8,128)(2,1)S(1)}, u32[]{:S(2)}, u32[]{:S(2)}) async-start(bf16[8,512,128]{2,1,0:T(8,128)(2,1)} %bitcast.66), calls=%async_computation.1 | async-start | bytes 2097152 | tf_op jit(solution)/shard_map/all_to_all | solution.py:562
  231.9 13.0 %copy-start.3 = (bf16[4096,128]{1,0:T(8,128)(2,1)S(1)}, bf16[4096,128]{1,0:T(8,128)(2,1)}, u32[]{:S(2)}) copy-start(bf16[4096,128]{1,0:T(8,128)(2,1)} %copy-done.2) | copy-start | bytes 3145732
  244.9 1.2 copy-start.5
  467.1 3.7 copy-start.9
  467.1 4.7 copy-start.13
  470.8 1.8 copy-start.8
Sparse Core Ops, SparseCore 0:
  10.4 107.5 all-gather.3
  119.8 45.2 all-gather.5
  167.0 42.8 all-gather.7
  213.3 195.8 reduce-scatter.1
where the time goes:
time: 487 us; the launch traced here: 481 us
  Pallas kernels  347 us (71%)
  matrix products  62.6 us (13%)
  local copies, waits for them, and re-layouts  23.5 us (5%)
  waiting for transfers between devices  23 us (5%)
  between operations  14.5 us (3%)
  starting transfers between devices  5.66 us (1%)
    pallas_call x1, Pallas kernels, tail_stage(): pl.pallas_call(tail_kernel, out_shape=(jax.ShapeDtypeStruct((DN_ROWS, D),...  168 us
    pallas_call x1, Pallas kernels, head_stage(): pl.pallas_call(head_kernel, out_shape=(jax.ShapeDtypeStruct((SEQ, D), BF1...  101 us
    pallas_call x1, Pallas kernels, attn_backward(): pl.pallas_call(attn_bwd_kernel, out_shape=jax.ShapeDtypeStruct((SEQ, 3 *...  47.2 us
    pallas_call x1, Pallas kernels, attn_forward(): pl.pallas_call(attn_fwd_kernel, out_shape=(jax.ShapeDtypeStruct((SEQ, LAN...  31.4 us
    dot_general x3, matrix products, dot_nt(): lax.dot_general(a, b, (((1,), (1,)), ((), ())), preferred_element_type=F32)  23.2 us
    all_to_all x2, waiting for transfers between devices, exchange(): return lax.all_to_all(t, 'sp', 0, 0)  22.2 us
    dot_general x1, matrix products, dot_tn(): lax.dot_general(a, b, (((0,), (0,)), ((), ())), preferred_element_type=F32)  13.6 us
    dot_general x1, matrix products, local_layer(): gate_up = jnp.dot(z_norm, wgu_full, preferred_element_type=F32)  12.3 us
  transfers between devices with their start and end apart: 6, of which 2 were waited for; matrix products, arithmetic and copies ran while one was open for 16% of the time, Pallas kernels for 72%

commit v1 on v0

--- a/solution.py
+++ b/solution.py
@@ -542,6 +542,91 @@
     )(m_t, grad_y, o_t, grad_h, d_qkv, x, h_res, grad_z, gain1, u_all, win_full)
 
 
+def pair_grad_kernel(z_ref, g_ref, out_hbm, z_mate, g_mate, zt, acc, z_send, z_recv, g_send, g_recv, out_sem):
+    me = lax.axis_index('sp')
+    core = lax.rem(me, 2)
+    mate = me + 1 - 2 * core
+    blocks = g_ref.shape[1] // COLS
+    barrier = pltpu.get_barrier_semaphore()
+    pl.semaphore_signal(barrier, inc=1, device_id=(mate,), device_id_type=pl.DeviceIdType.MESH)
+    pl.semaphore_wait(barrier, 1)
+
+    def swap(src, dst, send_sem, recv_sem):
+        return pltpu.make_async_remote_copy(src_ref=src, dst_ref=dst, send_sem=send_sem, recv_sem=recv_sem,
+                                            device_id=(mate,), device_id_type=pl.DeviceIdType.MESH)
+
+    def block(b):
+        return pl.ds(pl.multiple_of(b * COLS, COLS), COLS)
+
+    def g_swap(b):
+        return swap(g_ref.at[:, block(b)], g_mate.at[:, block(b)], g_send.at[b], g_recv.at[b])
+
+    def out_copy(b):
+        slot = lax.rem(b, 2)
+        return pltpu.make_async_copy(acc.at[slot], out_hbm.at[:, block(b)], out_sem.at[slot])
+
+    z_swap = swap(z_ref, z_mate, z_send, z_recv)
+    z_swap.start()
+
+    def start_swap(b, _):
+        g_swap(b).start()
+        return 0
+
+    lax.fori_loop(0, blocks, start_swap, 0)
+
+    def dest_cols(q):
+        return pl.ds(pl.multiple_of((2 * q + core) * LANES, LANES), LANES)
+
+    for q in range(NDEV // 2):
+        zt[q * LANES:(q + 1) * LANES, 0:TOK] = z_ref[:, dest_cols(q)].T
+    z_swap.wait_recv()
+    for q in range(NDEV // 2):
+        zt[q * LANES:(q + 1) * LANES, TOK:2 * TOK] = z_mate[:, dest_cols(q)].T
+
+    def one_block(b, _):
+        slot = lax.rem(b, 2)
+
+        @pl.when(b >= 2)
+        def _():
+            out_copy(b - 2).wait()
+
+        g_swap(b).wait_recv()
+        acc[slot] = (jnp.dot(zt[:, 0:TOK], g_ref[:, block(b)], preferred_element_type=F32)
+                     + jnp.dot(zt[:, TOK:2 * TOK], g_mate[:, block(b)], preferred_element_type=F32))
+        out_copy(b).start()
+        return 0
+
+    lax.fori_loop(0, blocks, one_block, 0)
+    out_copy(blocks - 2).wait()
+    out_copy(blocks - 1).wait()
+
+    def end_swap(b, _):
+        g_swap(b).wait_send()
+        return 0
+
+    lax.fori_loop(0, blocks, end_swap, 0)
+    z_swap.wait_send()
+
+
+def pair_grad(z, grad_gu):
+    dma = pltpu.SemaphoreType.DMA
+    width = grad_gu.shape[1]
+    blocks = width // COLS
+    return pl.pallas_call(
+        pair_grad_kernel,
+        out_shape=jax.ShapeDtypeStruct((D // 2, width), F32),
+        in_specs=[VMEM_SPEC] * 2,
+        out_specs=pl.BlockSpec(memory_space=pl.ANY),
+        scratch_shapes=[pltpu.VMEM((TOK, D), BF16), pltpu.VMEM((TOK, width), BF16),
+                        pltpu.VMEM((D // 2, 2 * TOK), BF16), pltpu.VMEM((2, D // 2, COLS), F32),
+                        dma, dma, dma((blocks,)), dma((blocks,)), dma((2,))],
+        compiler_params=pltpu.CompilerParams(collective_id=2, has_side_effects=True,
+                                             vmem_limit_bytes=60 * 1024 * 1024),
+        cost_estimate=pl.CostEstimate(flops=6_000_000_000, bytes_accessed=20_000_000, transcendentals=0),
+        name='pair_grad',
+    )(z, grad_gu)
+
+
 def rms_back(grad_out, normed, inv_rms):
     mean_term = jnp.mean(grad_out * normed, axis=-1, keepdims=True)
     return inv_rms * (grad_out - normed * mean_term)
@@ -554,9 +639,6 @@
 
     def gather(t):
         return lax.all_gather(t, 'sp', axis=0, tiled=True)
-
-    def scatter_sum(t):
-        return lax.psum_scatter(t, 'sp', scatter_dimension=0, tiled=True)
 
     def exchange(t):
         return lax.all_to_all(t, 'sp', 0, 0)
@@ -598,7 +680,8 @@
         grad_gate = (grad_act * up_pre * gate_sig * (1.0 + gate_pre * (1.0 - gate_sig))).astype(BF16)
         grad_up = (grad_act * gate_act).astype(BF16)
         grad_gu = jnp.concatenate([grad_gate, grad_up], axis=1)
-        grad_wgu = scatter_sum(dot_tn(z_norm, grad_gu))
+        grad_wgu = lax.psum_scatter(pair_grad(z_norm, grad_gu), 'sp', scatter_dimension=0, tiled=True,
+                                    axis_index_groups=[[0, 2, 4, 6], [1, 3, 5, 7]])
         grad_z_b = lax.optimization_barrier(dot_nt(grad_gu, wgu_full).astype(BF16))
         grad_z = grad_z_b.astype(F32)
         grad_h = (grad_y.astype(F32) + rms_back(grad_z * gain2, normed2, inv_rms2)).astype(BF16)

time: 487 us -> 476 us (0.977); the launches traced: 481 us -> 476 us
  matrix products: 62.6 us -> 50.4 us
  Pallas kernels: 347 us -> 337 us
  waiting for transfers between devices: 23 us -> 32.2 us
    pallas_call x1, Pallas kernels: 168 us -> 140 us  [tail_stage(): pl.pallas_call(tail_kernel, out_shape=(jax.ShapeDtypeStruct((DN_ROWS, D),...]
    pallas_call x0 -> x1, Pallas kernels: none -> 17.1 us  [pair_grad(): pl.pallas_call(pair_grad_kernel, out_shape=jax.ShapeDtypeStruct((D // 2,...]
    dot_general x1 -> x0, matrix products: 13.6 us -> none  [dot_tn(): lax.dot_general(a, b, (((0,), (0,)), ((), ())), preferred_element_type=F32)]
    all_to_all x2, waiting for transfers between devices: 22.2 us -> 31.4 us  [exchange(): return lax.all_to_all(t, 'sp', 0, 0)]
  transfers between devices with their start and end apart: 6 -> 6, of which waited for: 2 -> 2; matrix products, arithmetic and copies ran while one was open for 16% -> 15% of each run, Pallas kernels for 72% -> 71%
where the time goes in v1:
time: 476 us
  Pallas kernels  337 us (71%)
  matrix products  50.4 us (11%)
  waiting for transfers between devices  32.2 us (7%)
  local copies, waits for them, and re-layouts  28.2 us (6%)
  between operations  14.2 us (3%)
  other arithmetic  8.18 us (2%)
  starting transfers between devices  5.25 us (1%)
    pallas_call x1, Pallas kernels, tail_stage(): pl.pallas_call(tail_kernel, out_shape=(jax.ShapeDtypeStruct((DN_ROWS, D),...  140 us
    pallas_call x1, Pallas kernels, head_stage(): pl.pallas_call(head_kernel, out_shape=(jax.ShapeDtypeStruct((SEQ, D), BF1...  102 us
    pallas_call x1, Pallas kernels, attn_backward(): pl.pallas_call(attn_bwd_kernel, out_shape=jax.ShapeDtypeStruct((SEQ, 3 *...  47.1 us
    all_to_all x2, waiting for transfers between devices, exchange(): return lax.all_to_all(t, 'sp', 0, 0)  31.4 us
    pallas_call x1, Pallas kernels, attn_forward(): pl.pallas_call(attn_fwd_kernel, out_shape=(jax.ShapeDtypeStruct((SEQ, LAN...  31.4 us
    dot_general x3, matrix products, dot_nt(): lax.dot_general(a, b, (((1,), (1,)), ((), ())), preferred_element_type=F32)  25.1 us
    pallas_call x1, Pallas kernels, pair_grad(): pl.pallas_call(pair_grad_kernel, out_shape=jax.ShapeDtypeStruct((D // 2,...  17.1 us
    dot_general x1, matrix products, local_layer(): gate_up = jnp.dot(z_norm, wgu_full, preferred_element_type=F32)  14.1 us
  transfers between devices with their start and end apart: 6, of which 2 were waited for; matrix products, arithmetic and copies ran while one was open for 15% of the time, Pallas kernels for 71%

profile of v1, /device:TPU:0, one launch (start us, length us, event | category | flops | bytes accessed | tf_op | source)
XLA Modules:
  0.0 475.8 jit_solution(12924088286241120218)
XLA Ops:
  7.3 2.6 pad_maximum_fusion.1
  12.0 1.1 fusion.19
  13.1 1.0 copy.38
  14.4 101.8 %head_stage.1 = (bf16[4096,1024]{1,0:T(8,128)(2,1)}, bf16[4096,128]{1,0:T(8,128)(2,1)S(1)}, bf16[4096,128]{1,0:T(8,128)(2,1)S(1)}, bf16[4096,128]{1,0:T(8,128)(2...) custom-call(bf16[512,1024]{1,0:T(8,128)(2,1)S(1)} %copy-done, ...), custom_call_target="tpu_custom_call" | custom-call | flops 40000000000 | bytes 30000000 | tf_op jit(solution)/shard_map/head_stage/pallas_call | solution.py:327
  116.3 31.4 %attn_fwd.1 = (bf16[4096,128]{1,0:T(8,128)(2,1)}, f32[16,512]{1,0:T(8,128)S(1)}) custom-call(s32[16,512]{1,0:T(8,128)S(1)} %get-tuple-element.27.lo_ref.start_ref, s32[16,512]{1,0:T(8,128)S(1)} %get-tuple-element.27.lo_ref.start_ref, bf16[4096,128]{1,0:T(8,128)(2,1)S(1)} %get-tuple-element.28.q_ref, bf16[4096,128]{1,0:T(8,128)(2,1)S(1)} %get-tuple-element.29.k_ref, ...), custom_call_target="tpu_custom_call" | custom-call | flops 20000000000 | bytes 5000000 | tf_op jit(solution)/shard_map/attn_fwd/pallas_call | solution.py:142
  147.6 2.4 all-to-all-start
  150.8 18.7 %all-to-all-done = bf16[8,512,128]{2,1,0:T(8,128)(2,1)S(1)} async-done(((bf16[8,512,128]{2,1,0:T(8,128)(2,1)}), bf16[8,512,128]{2,1,0:T(8,128)(2,1)S(1)}, u32[]{:S(2)}, u32[]{:S(2)}) %all-to-all-start) | async-done | bytes 1048608 | tf_op jit(solution)/shard_map/all_to_all | solution.py:644
  170.5 3.3 fusion.14
  174.2 14.1 %fusion.22 = f32[512,5632]{1,0:T(8,128)} fusion(bf16[512,1024]{1,0:T(8,128)(2,1)S(1)} %fusion.8.z_ref, bf16[1024,5632]{1,0:T(8,128)(2,1)} %all-gather.4.cloned.1.call-done), kind=kOutput, calls=%fused_computation.51 | convolution fusion | flops 5905580032 | bytes 24117248 | tf_op jit(solution)/shard_map/dot_general | solution.py:673
  188.2 12.2 %fusion.2 = (bf16[512,2816]{1,0:T(8,128)(2,1)S(1)}, bf16[512,2816]{1,0:T(8,128)(2,1)S(1)}, bf16[512,2816]{1,0:T(8,128)(2,1)}) fusion(f32[512,5632]{1,0:T(8,128)} %fusion.22, bf16[512,1024]{1,0:T(8,128)(2,1)} %gy_ref.1, bf16[2816,1024]{1,0:T(8,128)(2,1)} %all-gather.6.cloned.1.call-done), kind=kOutput, calls=%fused_computation.4 | convolution fusion | flops 2977300480 | bytes 27000832 | tf_op jit(solution)/shard_map/dot_general | solution.py:27
  200.4 1.6 copy-done.10
  202.0 1.0 copy-done.11
  203.0 2.9 pad_maximum_fusion.g_ref
  205.9 17.1 %pair_grad.1 = f32[512,5632]{1,0:T(8,128)} custom-call(bf16[512,1024]{1,0:T(8,128)(2,1)} %copy-done.13, bf16[512,5632]{1,0:T(8,128)(2,1)} %pad_maximum_fusion.g_ref), custom_call_target="tpu_custom_call" | custom-call | flops 6000000000 | bytes 20000000 | tf_op jit(solution)/shard_map/pair_grad/pallas_call | solution.py:615
  223.0 11.6 %convolution_convert_fusion.1.gz_ref = bf16[512,1024]{1,0:T(8,128)(2,1)S(1)} fusion(bf16[1024,5632]{1,0:T(8,128)(2,1)} %all-gather.4.cloned.1.call-done, bf16[512,2816]{1,0:T(8,128)(2,1)} %copy-done.11, bf16[512,2816]{1,0:T(8,128)(2,1)} %copy-done.10), kind=kOutput, calls=%fused_computation.28 | convolution fusion | flops 5917638656 | bytes 18350080 | tf_op jit(solution)/shard_map/dot_general | solution.py:27
  236.6 1.3 fusion.17
  237.9 1.2 copy.40
  239.1 2.5 all-to-all-start.1
  241.7 1.3 copy.30
  243.0 4.7 copy.33.mt_ref
  247.7 7.9 %fusion.15 = bf16[512,1024]{1,0:T(8,128)(2,1)} fusion(bf16[512,1024]{1,0:T(8,128)(2,1)} %copy-done.6, bf16[512,2816]{1,0:T(8,128)(2,1)} %get-tuple-element.45, bf16[2816,1024]{1,0:T(8,128)(2,1)} %all-gather.6.cloned.1.call-done), kind=kOutput, calls=%fused_computation.24 | convolution fusion | flops 2954362880 | bytes 10747904 | tf_op jit(solution)/shard_map/dot_general | solution.py:690
  255.6 12.7 %all-to-all-done.1 = bf16[8,512,128]{2,1,0:T(8,128)(2,1)S(1)} async-done(((bf16[8,512,128]{2,1,0:T(8,128)(2,1)}), bf16[8,512,128]{2,1,0:T(8,128)(2,1)S(1)}, u32[]{:S(2)}, u32[]{:S(2)}) %all-to-all-start.1) | async-done | bytes 1048608 | tf_op jit(solution)/shard_map/all_to_all | solution.py:644
  268.4 1.4 copy-done.5
  269.7 47.1 %attn_bwd.1 = bf16[4096,384]{1,0:T(8,128)(2,1)} custom-call(s32[16,512]{1,0:T(8,128)S(1)} %get-tuple-element.27.lo_ref.start_ref, s32[16,512]{1,0:T(8,128)S(1)} %get-tuple-element.27.lo_ref.start_ref, f32[16,512]{1,0:T(8,128)S(1)} %get-tuple-element.34.lse_ref, bf16[4096,128]{1,0:T(8,128)(2,1)S(1)} %get-tuple-element.28.q_ref, ...), custom_call_target="tpu_custom_call" | custom-call | flops 49999998976 | bytes 12000000 | tf_op jit(solution)/shard_map/attn_bwd/pallas_call | solution.py:155
  316.8 140.1 %tail_stage.1 = (f32[352,1024]{1,0:T(8,128)}, f32[128,1024]{1,0:T(8,128)}, f32[8,128,384]{2,1,0:T(8,128)}, bf16[512,1024]{1,0:T(8,128)(2,1)}, f32[8,128]{1,0:T(8,128)}) custom-call(bf16[2816,512]{1,0:T(8,128)(2,1)} %copy.33.mt_ref, bf16[512,1024]{1,0:T(8,128)(2,1)} %gy_ref.1, bf16[1024,512]{1,0:T(8,128)(2,1)} %bitcast.74, bf16[512,1024]{1,0:T(8,128)(2,1)} %copy-done.16, ...), custom_call_target="tpu_custom_call" | custom-call | flops 60000002048 | bytes 60000000 | tf_op jit(solution)/shard_map/tail_stage/pallas_call | solution.py:523
  456.9 1.5 slice_bitcast_fusion
  458.5 1.0 copy.34
  459.5 1.0 copy.35
  460.4 1.0 copy.36
  461.4 1.3 slice_bitcast_fusion.4
  462.7 3.7 fusion.21
  468.2 1.1 copy.46
  (77 shorter events, 8.2 us)
Async XLA Ops:
  7.2 3.5 copy-start.18
  7.2 3.7 copy-start.19
  7.2 3.9 copy-start.20
  7.2 166.9 %all-gather.4.cloned.1.call-start = ((), (), s32[]{:S(2)}) async-start(), calls=%async_computation.3 | async-start | bytes 12976128 | tf_op jit(solution)/shard_map/all_gather | solution.py:641
  9.9 178.4 %all-gather.6.cloned.1.call-start = ((), (), s32[]{:S(2)}) async-start(), calls=%async_computation.4 | async-start | bytes 6488064 | tf_op jit(solution)/shard_map/all_gather | solution.py:641
  10.6 306.2 %all-gather.8.cloned.1.call-start = ((), (), s32[]{:S(2)}) async-start(), calls=%async_computation.5 | async-start | bytes 7077888 | tf_op jit(solution)/shard_map/all_gather | solution.py:641
  10.9 3.2 copy-start.21
  10.9 3.3 copy-start.22
  10.9 3.2 copy-start.23
  10.9 3.5 copy-start
  10.9 3.5 copy-start.1
  116.2 31.4 %copy-start.2 = (bf16[4096,128]{1,0:T(8,128)(2,1)}, bf16[4096,128]{1,0:T(8,128)(2,1)S(1)}, u32[]{:S(2)}) copy-start(bf16[4096,128]{1,0:T(8,128)(2,1)S(1)} %get-tuple-element.29.k_ref) | copy-start | bytes 3145732
  116.2 31.4 %copy-start.4 = (bf16[4096,128]{1,0:T(8,128)(2,1)}, bf16[4096,128]{1,0:T(8,128)(2,1)S(1)}, u32[]{:S(2)}) copy-start(bf16[4096,128]{1,0:T(8,128)(2,1)S(1)} %get-tuple-element.30.v_ref) | copy-start | bytes 3145732
  147.6 21.9 %all-to-all-start = ((bf16[8,512,128]{2,1,0:T(8,128)(2,1)}), bf16[8,512,128]{2,1,0:T(8,128)(2,1)S(1)}, u32[]{:S(2)}, u32[]{:S(2)}) async-start(bf16[8,512,128]{2,1,0:T(8,128)(2,1)} %bitcast.8), calls=%async_computation | async-start | bytes 2097152 | tf_op jit(solution)/shard_map/all_to_all | solution.py:644
  150.0 312.7 %reduce-scatter.2.cloned.1.call-start = ((), (), s32[]{:S(2)}) async-start(), calls=%async_computation.6 | async-start | bytes 14417920 | tf_op jit(solution)/shard_map/reduce_scatter | solution.py:683
  169.5 1.0 copy-start.7
  173.8 61.4 %copy-start.6 = (bf16[512,1024]{1,0:T(8,128)(2,1)}, bf16[512,1024]{1,0:T(8,128)(2,1)S(1)}, u32[]{:S(2)}) copy-start(bf16[512,1024]{1,0:T(8,128)(2,1)S(1)} %get-tuple-element.58.h_ref) | copy-start | bytes 3145732
  174.1 14.1 %copy-start.13 = (bf16[512,1024]{1,0:T(8,128)(2,1)}, bf16[512,1024]{1,0:T(8,128)(2,1)S(1)}, u32[]{:S(2)}) copy-start(bf16[512,1024]{1,0:T(8,128)(2,1)S(1)} %fusion.8.z_ref) | copy-start | bytes 3145732
  200.4 1.6 copy-start.10
  200.4 2.6 copy-start.11
  223.0 12.2 %copy-start.15 = (bf16[512,1024]{1,0:T(8,128)(2,1)S(1)}, bf16[512,1024]{1,0:T(8,128)(2,1)}, u32[]{:S(2)}) copy-start(bf16[512,1024]{1,0:T(8,128)(2,1)} %gy_ref.1) | copy-start | bytes 3145732
  234.6 1.3 copy-start.9
  234.7 2.0 copy-start.24
  235.9 2.0 copy-start.16
  237.9 3.7 copy-start.8
  239.1 29.2 %all-to-all-start.1 = ((bf16[8,512,128]{2,1,0:T(8,128)(2,1)}), bf16[8,512,128]{2,1,0:T(8,128)(2,1)S(1)}, u32[]{:S(2)}, u32[]{:S(2)}) async-start(bf16[8,512,128]{2,1,0:T(8,128)(2,1)} %bitcast.71), calls=%async_computation.1 | async-start | bytes 2097152 | tf_op jit(solution)/shard_map/all_to_all | solution.py:644
  247.7 20.7 %copy-start.3 = (bf16[4096,128]{1,0:T(8,128)(2,1)S(1)}, bf16[4096,128]{1,0:T(8,128)(2,1)}, u32[]{:S(2)}) copy-start(bf16[4096,128]{1,0:T(8,128)(2,1)} %copy-done.2) | copy-start | bytes 3145732
  268.4 1.4 copy-start.5
  462.7 3.7 copy-start.14
  462.7 4.7 copy-start.17
  466.4 1.8 copy-start.12
Sparse Core Ops, SparseCore 0:
  10.4 109.1 all-gather.3
  121.4 44.3 all-gather.5
  167.6 43.4 all-gather.7
  223.1 148.5 reduce-scatter.1

commit v2 on v0

--- a/solution.py
+++ b/solution.py
@@ -218,19 +218,14 @@
     for c in smalls + weights:
         c.wait_recv()
 
-    lane = lax.broadcasted_iota(jnp.int32, (LANES, LANES), 1)
-    first_half = lax.rem(lane, HD) < HD // 2
-
-    def build(i, _):
-        rows = pl.ds(pl.multiple_of(i * LANES, LANES), LANES)
-        w_ext[rows, 0:3 * LANES] = w_buf[i]
-        for n in range(2):
-            t = w_buf[i, :, n * LANES:(n + 1) * LANES].astype(F32)
-            rot = jnp.where(first_half, -pltpu.roll(t, LANES - HD // 2, 1), pltpu.roll(t, HD // 2, 1))
-            w_ext[rows, (3 + n) * LANES:(4 + n) * LANES] = rot.astype(BF16)
-        return 0
-
-    lax.fori_loop(0, NDEV, build, 0)
+    half_head = HD // 2
+    for n in range(NDEV):
+        cols = slice(n * LANES, (n + 1) * LANES)
+        w_ext[0:3 * LANES, cols] = w_buf[n]
+        for m in range(2):
+            t = w_buf[n, m * LANES:(m + 1) * LANES, :].astype(F32)
+            rot = jnp.concatenate([-t[half_head:HD], t[:half_head], -t[HD + half_head:], t[HD:HD + half_head]], axis=0)
+            w_ext[(3 + m) * LANES:(4 + m) * LANES, cols] = rot.astype(BF16)
     gain1 = jnp.concatenate([all_small[n, 0:1, :] for n in range(NDEV)], axis=1)
 
     def process(order, src_ref, src_dev, h):
@@ -241,7 +236,7 @@
             inv = lax.rsqrt(jnp.mean(xv * xv, axis=-1, keepdims=True) + NORM_EPS)
             u = (xv * inv * gain1).astype(BF16)
             u_buf[rows, :] = u
-            proj = jnp.dot(u, w_ext[...], preferred_element_type=F32)
+            proj = dot_nt(u, w_ext[...])
             angle = freq_ref[...] * all_small[src_dev, pl.ds(2 + 2 * h + i, 1), :]
             cos4, sin4 = jnp.cos(angle), jnp.sin(angle)
             cos_v = jnp.concatenate([cos4] * 4, axis=0).T
@@ -332,8 +327,8 @@
            jax.ShapeDtypeStruct((NDEV, LANES, D), BF16)),
         in_specs=[VMEM_SPEC] * 5,
         out_specs=(pl.BlockSpec(memory_space=pl.ANY),) + (VMEM_SPEC,) * 8,
-        scratch_shapes=[pltpu.VMEM((NDEV, TOK, D), BF16), pltpu.VMEM((NDEV, LANES, 3 * LANES), BF16),
-                        pltpu.VMEM((D, 5 * LANES), BF16), pltpu.VMEM((SEQ, D), BF16),
+        scratch_shapes=[pltpu.VMEM((NDEV, TOK, D), BF16), pltpu.VMEM((NDEV, 3 * LANES, LANES), BF16),
+                        pltpu.VMEM((5 * LANES, D), BF16), pltpu.VMEM((SEQ, D), BF16),
                         dma((NDEV - 1,)), dma((NDEV - 1,)), dma((NDEV - 1,)), dma((NDEV - 1,)),
                         dma((14,)), dma((14,)), dma((14,)), dma((14,)), dma((16,))],
         compiler_params=pltpu.CompilerParams(collective_id=0, has_side_effects=True,
@@ -349,9 +344,9 @@
 
 
 def tail_kernel(mt_ref, gy_ref, ot_ref, gh_ref, d_ref, x_ref, h_ref, gz_ref, gain_ref, u_hbm, win_hbm,
-                dn_out, wo_out, gw_out, gx_out, gain_out,
-                mt_mate, gy_mate, ot_mate, gh_mate, part, box, d_buf, win_buf, u_buf, gw_mine, gain_mine, gain_buf,
-                mate_send, mate_recv, rs_send, rs_recv, d_send, d_recv, gw_send, gw_recv, gg_send, gg_recv, win_sem, u_sem):
+                dn_out, wo_out, gq_out, gk_out, gv_out, gx_out, gain_out,
+                mt_mate, gy_mate, ot_mate, gh_mate, part, box, d_buf, win_buf, u_buf, gw_acc, gw_in, gain_mine, gain_buf,
+                mate_send, mate_recv, rs_send, rs_recv, d_send, d_recv, gw_send, gw_recv, gg_send, gg_recv, win_send, win_recv, win_sem, u_sem):
     me = lax.axis_index('sp')
     core = lax.rem(me, 2)
     x_pos = lax.rem(me // 2, 2)
@@ -359,8 +354,12 @@
     step_c, step_x, step_y = 1 - 2 * core, 2 - 4 * x_pos, 4 - 8 * y_pos
     mate, near_x, near_y, diag = me + step_c, me + step_x, me + step_y, me + step_x + step_y
 
-    win_copy = pltpu.make_async_copy(win_hbm, win_buf, win_sem)
-    win_copy.start()
+    def win_part(q):
+        return win_buf.at[:, pl.ds(pl.multiple_of((2 * q + core) * LANES, LANES), LANES)]
+
+    win_copies = [pltpu.make_async_copy(win_hbm.at[q], win_part(q), win_sem.at[q]) for q in range(NDEV // 2)]
+    for c in win_copies:
+        c.start()
     u_copy = pltpu.make_async_copy(u_hbm, u_buf, u_sem)
     u_copy.start()
 
@@ -393,9 +392,17 @@
     for c in swaps:
         c.start()
     d_moves = to_peers(d_ref, d_buf, d_send, d_recv)
-    gw_moves = to_peers(gw_mine, gw_out, gw_send, gw_recv)
+
+    def gw_cols(dev):
+        return gw_acc.at[:, pl.ds(pl.multiple_of(dev * LANES, LANES), LANES)]
+
+    gw_moves = [remote(gw_cols(lax.rem(me + n, NDEV)), gw_in.at[me], gw_send.at[n - 1], gw_recv.at[n - 1],
+                       lax.rem(me + n, NDEV)) for n in range(1, NDEV)]
     gg_moves = to_peers(gain_mine, gain_buf, gg_send, gg_recv)
     for c in d_moves:
+        c.start()
+    win_swaps = [remote(win_hbm.at[q], win_part(q), win_send.at[q], win_recv.at[q], mate) for q in range(NDEV // 2)]
+    for c in win_swaps:
         c.start()
     d_buf[me] = d_ref[me]
     for c in swaps:
@@ -429,18 +436,16 @@
     compute(1, near_x, 1)
     u_copy.wait()
 
-    def grad_win_piece(n, _):
-        cols = pl.ds(pl.multiple_of(n * LANES, LANES), LANES)
-        total = dot_tn(u_buf[0:TOK, cols], d_ref[0])
-        for g in range(1, NDEV):
-            total = total + dot_tn(u_buf[g * TOK:(g + 1) * TOK, cols], d_ref[g])
-        gw_mine[n] = total
-        return 0
-
-    lax.fori_loop(0, NDEV, grad_win_piece, 0)
+    gw_acc[...] = dot_tn(d_ref[0], u_buf[0:TOK, :])
+
+    def grad_win_part(g, _):
+        gw_acc[...] += dot_tn(d_ref[g], u_buf[pl.ds(pl.multiple_of(g * TOK, TOK), TOK), :])
+        return 0
+
+    lax.fori_loop(1, NDEV, grad_win_part, 0)
     for c in gw_moves:
         c.start()
-    gw_out[me] = gw_mine[me]
+    gw_in[me] = gw_acc[:, pl.ds(pl.multiple_of(me * LANES, LANES), LANES)]
     compute(0, me, 0)
     compute(0, me, 1)
 
@@ -461,15 +466,19 @@
 
     for c in d_moves:
         c.wait_recv()
-    win_copy.wait()
+    for c in win_copies:
+        c.wait()
+    for c in win_swaps:
+        c.wait_recv()
     gain1 = gain_ref[...]
 
     def grad_rows(i, carry):
         acc, acc2 = carry
         rows = pl.ds(pl.multiple_of(i * LANES, LANES), LANES)
-        gu = dot_nt(d_buf[0, rows, :], win_buf[:, 0:3 * LANES])
+        gu = jnp.dot(d_buf[0, rows, :], win_buf[0:3 * LANES, :], preferred_element_type=F32)
         for g in range(1, NDEV):
-            gu = gu + dot_nt(d_buf[g, rows, :], win_buf[:, g * 3 * LANES:(g + 1) * 3 * LANES])
+            gu = gu + jnp.dot(d_buf[g, rows, :], win_buf[g * 3 * LANES:(g + 1) * 3 * LANES, :],
+                              preferred_element_type=F32)
         gu = gu.astype(BF16).astype(F32)
         xv = x_ref[rows, :].astype(F32)
         inv = lax.rsqrt(jnp.mean(xv * xv, axis=-1, keepdims=True) + NORM_EPS)
@@ -513,7 +522,9 @@
         wo_out[:, col * COLS:(col + 1) * COLS] = part[0, col, DN_ROWS:OUT_ROWS, :] + box[4 + col, DN_ROWS:OUT_ROWS, :]
     for c in gw_moves:
         c.wait_recv()
-    for c in swaps + d_moves + gw_moves + gg_moves + moves:
+    for n, ref in enumerate((gq_out, gk_out, gv_out)):
+        ref[...] = gw_in[:, n * LANES:(n + 1) * LANES, :]
+    for c in swaps + d_moves + gw_moves + gg_moves + moves + win_swaps:
         c.wait_send()
 
 
@@ -523,18 +534,18 @@
     return pl.pallas_call(
         tail_kernel,
         out_shape=(jax.ShapeDtypeStruct((DN_ROWS, D), F32), jax.ShapeDtypeStruct((LANES, D), F32),
-                   jax.ShapeDtypeStruct((NDEV, LANES, 3 * LANES), F32), jax.ShapeDtypeStruct((TOK, D), BF16),
+                   *(jax.ShapeDtypeStruct((NDEV, LANES, LANES), F32),) * 3, jax.ShapeDtypeStruct((TOK, D), BF16),
                    jax.ShapeDtypeStruct((8, LANES), F32)),
-        in_specs=[VMEM_SPEC] * 9 + [pl.BlockSpec(memory_space=pl.ANY)] * 2,
-        out_specs=(VMEM_SPEC,) * 5,
+        in_specs=[VMEM_SPEC] * 9 + [pl.BlockSpec(memory_space=pltpu.HBM)] * 2,
+        out_specs=(VMEM_SPEC,) * 7,
         scratch_shapes=[pltpu.VMEM((4, DN_ROWS, TOK), BF16), pltpu.VMEM((TOK, D), BF16),
                         pltpu.VMEM((4, LANES, TOK), BF16), pltpu.VMEM((TOK, D), BF16),
                         pltpu.VMEM((4, 2, OUT_ROWS, COLS), F32), pltpu.VMEM((6, OUT_ROWS, COLS), F32),
-                        pltpu.VMEM((NDEV, TOK, 3 * LANES), BF16), pltpu.VMEM((D, 3 * D), BF16),
-                        pltpu.VMEM((SEQ, D), BF16), pltpu.VMEM((NDEV, LANES, 3 * LANES), F32),
+                        pltpu.VMEM((NDEV, TOK, 3 * LANES), BF16), pltpu.VMEM((3 * D, D), BF16), pltpu.VMEM((SEQ, D), BF16),
+                        pltpu.VMEM((3 * LANES, D), F32), pltpu.VMEM((NDEV, 3 * LANES, LANES), F32),
                         pltpu.VMEM((NDEV, 8, LANES), F32), pltpu.VMEM((NDEV, 8, LANES), F32),
                         dma((10,)), dma((10,)), dma((6,)), dma((6,)), dma(peers), dma(peers),
-                        dma(peers), dma(peers), dma(peers), dma(peers), dma, dma],
+                        dma(peers), dma(peers), dma(peers), dma(peers), dma((4,)), dma((4,)), dma((4,)), dma],
         compiler_params=pltpu.CompilerParams(collective_id=1, has_side_effects=True,
                                              vmem_limit_bytes=60 * 1024 * 1024),
         cost_estimate=pl.CostEstimate(flops=60_000_000_000, bytes_accessed=60_000_000, transcendentals=1_000),
@@ -542,6 +553,148 @@
     )(m_t, grad_y, o_t, grad_h, d_qkv, x, h_res, grad_z, gain1, u_all, win_full)
 
 
+UP_COLS = 256
+DW_COLS = 512
+DZ_COLS = 1408
+SLOTS = 4
+
+
+def mlp_kernel(z_ref, gy_ref, wd_hbm, w_hbm, gz_out, mt_out, gw_hbm,
+               w_buf, wd_buf, g_buf, g_mate, z_mate, zt, acc, gz_acc,
+               swap_send, swap_recv, load_sem, wd_sem, z_send, z_recv, g_send, g_recv, out_sem):
+    me = lax.axis_index('sp')
+    core = lax.rem(me, 2)
+    mate = me + 1 - 2 * core
+    blocks = FF // UP_COLS
+    barrier = pltpu.get_barrier_semaphore()
+    pl.semaphore_signal(barrier, inc=1, device_id=(mate,), device_id_type=pl.DeviceIdType.MESH)
+    pl.semaphore_wait(barrier, 1)
+
+    def to_mate(src, dst, send_sem, recv_sem):
+        return pltpu.make_async_remote_copy(src_ref=src, dst_ref=dst, send_sem=send_sem, recv_sem=recv_sem,
+                                            device_id=(mate,), device_id_type=pl.DeviceIdType.MESH)
+
+    def cols(n, width):
+        return pl.ds(pl.multiple_of(n * width, LANES), width)
+
+    def w_swap(n):
+        return to_mate(w_hbm.at[:, :, cols(n, UP_COLS)], w_buf.at[:, core, :, cols(n, UP_COLS)],
+                       swap_send.at[n], swap_recv.at[n])
+
+    def w_load(n):
+        return pltpu.make_async_copy(w_hbm.at[:, :, cols(n, UP_COLS)], w_buf.at[:, core, :, cols(n, UP_COLS)],
+                                     load_sem.at[n])
+
+    def wd_load(b):
+        return pltpu.make_async_copy(wd_hbm.at[cols(b, UP_COLS), :], wd_buf.at[cols(b, UP_COLS), :], wd_sem.at[b])
+
+    def g_swap(n):
+        return to_mate(g_buf.at[:, cols(n, UP_COLS)], g_mate.at[:, cols(n, UP_COLS)], g_send.at[n], g_recv.at[n])
+
+    def out_copy(n):
+        slot = lax.rem(n, SLOTS)
+        return pltpu.make_async_copy(acc.at[slot], gw_hbm.at[:, cols(n, DW_COLS)], out_sem.at[slot])
+
+    def start(b, _):
+        for n in (b, b + blocks):
+            w_swap(n).start()
+            w_load(n).start()
+        wd_load(b).start()
+        return 0
+
+    lax.fori_loop(0, blocks, start, 0)
+    z_swap = to_mate(z_ref, z_mate, z_send, z_recv)
+    z_swap.start()
+
+    def dest_cols(q):
+        return pl.ds(pl.multiple_of((2 * q + core) * LANES, LANES), LANES)
+
+    for q in range(NDEV // 2):
+        zt[q * LANES:(q + 1) * LANES, 0:TOK] = z_ref[:, dest_cols(q)].T
+
+    def up_block(b, _):
+        for n in (b, b + blocks):
+            w_load(n).wait()
+            w_swap(n).wait_recv()
+        wd_load(b).wait()
+        rows = cols(b, UP_COLS)
+        low, high = cols(b, UP_COLS), cols(b + blocks, UP_COLS)
+        z = z_ref[...]
+        gate = jnp.dot(z, w_buf[:, :, :, low].reshape(D, UP_COLS), preferred_element_type=F32)
+        up = jnp.dot(z, w_buf[:, :, :, high].reshape(D, UP_COLS), preferred_element_type=F32)
+        g_act = dot_nt(gy_ref[...], wd_buf[rows, :]).astype(BF16).astype(F32)
+        sig = jax.nn.sigmoid(gate)
+        act = gate * sig
+        mt_out[rows, :] = (act * up).T.astype(BF16)
+        g_buf[:, low] = (g_act * up * sig * (1.0 + gate * (1.0 - sig))).astype(BF16)
+        g_buf[:, high] = (g_act * act).astype(BF16)
+        g_swap(b).start()
+        g_swap(b + blocks).start()
+        return 0
+
+    lax.fori_loop(0, blocks, up_block, 0)
+    z_swap.wait_recv()
+    for q in range(NDEV // 2):
+        zt[q * LANES:(q + 1) * LANES, TOK:2 * TOK] = z_mate[:, dest_cols(q)].T
+
+    def grad_block(n, _):
+        @pl.when(n >= SLOTS)
+        def _():
+            out_copy(n - SLOTS).wait()
+
+        g_swap(2 * n).wait_recv()
+        g_swap(2 * n + 1).wait_recv()
+        block = cols(n, DW_COLS)
+        acc[lax.rem(n, SLOTS)] = (jnp.dot(zt[:, 0:TOK], g_buf[:, block], preferred_element_type=F32)
+                                  + jnp.dot(zt[:, TOK:2 * TOK], g_mate[:, block], preferred_element_type=F32))
+        out_copy(n).start()
+        return 0
+
+    lax.fori_loop(0, blocks, grad_block, 0)
+    gz_acc[...] = jnp.zeros_like(gz_acc)
+
+    def gz_block(n, _):
+        block = cols(n, DZ_COLS)
+        gz_acc[...] += dot_nt(g_buf[:, block], w_buf[:, :, :, block].reshape(D, DZ_COLS))
+        return 0
+
+    lax.fori_loop(0, 2 * FF // DZ_COLS, gz_block, 0)
+    gz_out[...] = gz_acc[...].astype(BF16)
+    for n in range(blocks - SLOTS, blocks):
+        out_copy(n).wait()
+
+    def finish(n, _):
+        w_swap(n).wait_send()
+        g_swap(n).wait_send()
+        return 0
+
+    lax.fori_loop(0, 2 * blocks, finish, 0)
+    z_swap.wait_send()
+
+
+def mlp_stage(z, grad_y, wd_full, w_half):
+    dma = pltpu.SemaphoreType.DMA
+    count = 2 * FF // UP_COLS
+    hbm = pl.BlockSpec(memory_space=pltpu.HBM)
+    return pl.pallas_call(
+        mlp_kernel,
+        out_shape=(jax.ShapeDtypeStruct((TOK, D), BF16), jax.ShapeDtypeStruct((FF, TOK), BF16),
+                   jax.ShapeDtypeStruct((D // 2, 2 * FF), F32)),
+        in_specs=[VMEM_SPEC] * 2 + [hbm] * 2,
+        out_specs=(VMEM_SPEC, VMEM_SPEC, hbm),
+        scratch_shapes=[pltpu.VMEM((NDEV // 2, 2, LANES, 2 * FF), BF16), pltpu.VMEM((FF, D), BF16),
+                        pltpu.VMEM((TOK, 2 * FF), BF16), pltpu.VMEM((TOK, 2 * FF), BF16), pltpu.VMEM((TOK, D), BF16),
+                        pltpu.VMEM((D // 2, 2 * TOK), BF16), pltpu.VMEM((SLOTS, D // 2, DW_COLS), F32),
+                        pltpu.VMEM((TOK, D), F32),
+                        dma((count,)), dma((count,)), dma((count,)), dma((count // 2,)), dma, dma,
+                        dma((count,)), dma((count,)), dma((SLOTS,))],
+        compiler_params=pltpu.CompilerParams(collective_id=3, has_side_effects=True,
+                                             vmem_limit_bytes=58 * 1024 * 1024),
+        cost_estimate=pl.CostEstimate(flops=21_000_000_000, bytes_accessed=40_000_000, transcendentals=1_500_000),
+        name='mlp_stage',
+    )(z, grad_y, wd_full, w_half)
+
+
 def rms_back(grad_out, normed, inv_rms):
     mean_term = jnp.mean(grad_out * normed, axis=-1, keepdims=True)
     return inv_rms * (grad_out - normed * mean_term)
@@ -555,8 +708,11 @@
     def gather(t):
         return lax.all_gather(t, 'sp', axis=0, tiled=True)
 
-    def scatter_sum(t):
-        return lax.psum_scatter(t, 'sp', scatter_dimension=0, tiled=True)
+    same_core = [[0, 2, 4, 6], [1, 3, 5, 7]]
+
+    def gather_same_core(t):
+        full = lax.all_gather(t, 'sp', axis=0, tiled=True, axis_index_groups=same_core)
+        return full.reshape((NDEV // 2,) + t.shape)
 
     def exchange(t):
         return lax.all_to_all(t, 'sp', 0, 0)
@@ -567,9 +723,9 @@
         freq = jnp.broadcast_to(inv_freq, (half, LANES))
         small = jnp.concatenate([norm1_gain.astype(F32)[None, :], norm2_gain.astype(F32)[None, :],
                                  positions.astype(F32).reshape(4, LANES), jnp.zeros((2, LANES), F32)])
-        w_in = jnp.concatenate([t.reshape(LANES, NDEV, LANES) for t in (w_q, w_k, w_v)], axis=2)
+        w_in = jnp.concatenate([t.transpose(1, 2, 0).reshape(NDEV, LANES, LANES) for t in (w_q, w_k, w_v)], axis=1)
         u_all, q, k, v, cos_t, sin_t, small, start2, wo_full = head_stage(
-            x, w_in.transpose(1, 0, 2), small, freq, w_o.reshape(LANES, D))
+            x, w_in, small, freq, w_o.reshape(LANES, D))
         wo_full = wo_full.reshape(D, D)
         gain1 = small[:, 0].reshape(1, D)
         gain2 = small[:, 1].reshape(D)
@@ -579,8 +735,8 @@
         o_t = o_heads.transpose(0, 2, 1).reshape(D, TOK)
 
         wd_full = gather(w_down)
-        wgu_full = gather(jnp.concatenate([w_gate, w_up], axis=1))
-        win_full = gather(w_in.reshape(LANES, 3 * D))
+        wgu_half = gather_same_core(jnp.concatenate([w_gate, w_up], axis=1))
+        win_half = gather_same_core(w_in.reshape(3 * D, LANES))
 
         x_wide = x.astype(F32)
         h_res = (x_wide + jnp.dot(o_loc, wo_full, preferred_element_type=F32)).astype(BF16)
@@ -588,30 +744,19 @@
         inv_rms2 = lax.rsqrt(jnp.mean(h_wide * h_wide, axis=-1, keepdims=True) + NORM_EPS)
         normed2 = h_wide * inv_rms2
         z_norm = (normed2 * gain2).astype(BF16)
-        gate_up = jnp.dot(z_norm, wgu_full, preferred_element_type=F32)
-        gate_pre, up_pre = gate_up[:, :FF], gate_up[:, FF:]
-        gate_sig = jax.nn.sigmoid(gate_pre)
-        gate_act = gate_pre * gate_sig
-        mlp_act = (gate_act * up_pre).astype(BF16)
-
-        grad_act = dot_nt(grad_y, wd_full).astype(BF16).astype(F32)
-        grad_gate = (grad_act * up_pre * gate_sig * (1.0 + gate_pre * (1.0 - gate_sig))).astype(BF16)
-        grad_up = (grad_act * gate_act).astype(BF16)
-        grad_gu = jnp.concatenate([grad_gate, grad_up], axis=1)
-        grad_wgu = scatter_sum(dot_tn(z_norm, grad_gu))
-        grad_z_b = lax.optimization_barrier(dot_nt(grad_gu, wgu_full).astype(BF16))
+        grad_z_b, m_t, grad_wgu = mlp_stage(z_norm, grad_y, wd_full, wgu_half)
+        grad_wgu = lax.psum_scatter(grad_wgu, 'sp', scatter_dimension=0, tiled=True, axis_index_groups=same_core)
         grad_z = grad_z_b.astype(F32)
         grad_h = (grad_y.astype(F32) + rms_back(grad_z * gain2, normed2, inv_rms2)).astype(BF16)
         grad_o = dot_nt(grad_h, wo_full).astype(BF16)
         grad_o = exchange(grad_o.reshape(TOK, NDEV, LANES).transpose(1, 0, 2)).reshape(SEQ, LANES)
-        y = (h_wide + jnp.dot(mlp_act, wd_full, preferred_element_type=F32)).astype(BF16)
+        y = (h_wide + dot_tn(m_t, wd_full)).astype(BF16)
 
         d_qkv = attn_backward(start2, lse, q, k, v, o_own, grad_o, cos_t, sin_t)
-        grad_wdown, grad_wo, grad_win, grad_x, grad_gains = tail_stage(
-            mlp_act.T, grad_y, o_t, grad_h, d_qkv.reshape(NDEV, TOK, 3 * LANES), x, h_res, grad_z_b,
-            gain1, u_all, win_full)
-        grad_q, grad_k, grad_v = (grad_win[:, :, n * LANES:(n + 1) * LANES].transpose(1, 0, 2).reshape(LANES, 16, HD)
-                                  for n in range(3))
+        grad_wdown, grad_wo, *grad_qkv, grad_x, grad_gains = tail_stage(
+            m_t, grad_y, o_t, grad_h, d_qkv.reshape(NDEV, TOK, 3 * LANES), x, h_res, grad_z_b,
+            gain1, u_all, win_half)
+        grad_q, grad_k, grad_v = (t.reshape(16, HD, LANES).transpose(2, 0, 1) for t in grad_qkv)
         return (y, grad_x, grad_gains[0], grad_q, grad_k, grad_v, grad_wo.reshape(2, HD, D),
                 grad_gains[1], grad_wgu[:, :FF], grad_wgu[:, FF:], grad_wdown)
 

time: 487 us -> 459 us (0.943); the launches traced: 481 us -> 459 us
  matrix products: 62.6 us -> 12.9 us
  Pallas kernels: 347 us -> 366 us
  waiting for transfers between devices: 23 us -> 35.2 us
    pallas_call x0 -> x1, Pallas kernels: none -> 35.7 us  [mlp_stage(): pl.pallas_call(mlp_kernel, out_shape=(jax.ShapeDtypeStruct((TOK, D), BF16...]
    dot_general x2 -> x0, matrix products: 22.5 us -> none  [the longest x1 12.3 us: local_layer(): gate_up = jnp.dot(z_norm, wgu_full, preferred_element_type=F32)]
    dot_general x3 -> x1, matrix products: 23.2 us -> 1.29 us  [dot_nt(): lax.dot_general(a, b, (((1,), (1,)), ((), ())), preferred_element_type=F32)]
    pallas_call x1, Pallas kernels: 168 us -> 150 us  [tail_stage(): pl.pallas_call(tail_kernel, out_shape=(jax.ShapeDtypeStruct((DN_ROWS, D),...]
    all_to_all x2, waiting for transfers between devices: 22.2 us -> 34.4 us  [exchange(): return lax.all_to_all(t, 'sp', 0, 0)]
    dot_general x1, matrix products: 13.6 us -> 8.32 us  [dot_tn(): lax.dot_general(a, b, (((0,), (0,)), ((), ())), preferred_element_type=F32)]
    unnamed x49 -> x58, local copies, waits for them, and re-layouts: 8.31 us -> 11 us
  transfers between devices with their start and end apart: 6 -> 6, of which waited for: 2 -> 2; matrix products, arithmetic and copies ran while one was open for 16% -> 5% of each run, Pallas kernels for 72% -> 80%
where the time goes in v2:
time: 459 us
  Pallas kernels  366 us (80%)
  waiting for transfers between devices  35.2 us (8%)
  local copies, waits for them, and re-layouts  19.2 us (4%)
  between operations  14.1 us (3%)
  matrix products  12.9 us (3%)
  other arithmetic  6.18 us (1%)
  starting transfers between devices  5.14 us (1%)
    pallas_call x1, Pallas kernels, tail_stage(): pl.pallas_call(tail_kernel, out_shape=(jax.ShapeDtypeStruct((DN_ROWS, D),...  150 us
    pallas_call x1, Pallas kernels, head_stage(): pl.pallas_call(head_kernel, out_shape=(jax.ShapeDtypeStruct((SEQ, D), BF1...  101 us
    pallas_call x1, Pallas kernels, attn_backward(): pl.pallas_call(attn_bwd_kernel, out_shape=jax.ShapeDtypeStruct((SEQ, 3 *...  47.7 us
    pallas_call x1, Pallas kernels, mlp_stage(): pl.pallas_call(mlp_kernel, out_shape=(jax.ShapeDtypeStruct((TOK, D), BF16...  35.7 us
    all_to_all x2, waiting for transfers between devices, exchange(): return lax.all_to_all(t, 'sp', 0, 0)  34.4 us
    pallas_call x1, Pallas kernels, attn_forward(): pl.pallas_call(attn_fwd_kernel, out_shape=(jax.ShapeDtypeStruct((SEQ, LAN...  31.4 us
    unnamed x58, local copies, waits for them, and re-layouts  11 us
  transfers between devices with their start and end apart: 6, of which 2 were waited for; matrix products, arithmetic and copies ran while one was open for 5% of the time, Pallas kernels for 80%

profile of v2, /device:TPU:0, one launch (start us, length us, event | category | flops | bytes accessed | tf_op | source)
XLA Modules:
  0.0 458.9 jit_solution(10335044523200435180)
XLA Ops:
  7.3 2.6 pad_maximum_fusion
  9.9 0.7 all-gather.4.cloned.1.call-update
  10.7 1.0 pad_maximum_fusion.1.w_ref
  12.0 1.1 copy-done
  13.1 101.3 %head_stage.1 = (bf16[4096,1024]{1,0:T(8,128)(2,1)}, bf16[4096,128]{1,0:T(8,128)(2,1)S(1)}, bf16[4096,128]{1,0:T(8,128)(2,1)S(1)}, bf16[4096,128]{1,0:T(8,128)(2...) custom-call(bf16[512,1024]{1,0:T(8,128)(2,1)S(1)} %copy-done.1, ...), custom_call_target="tpu_custom_call" | custom-call | flops 40000000000 | bytes 30000000 | tf_op jit(solution)/shard_map/head_stage/pallas_call | solution.py:322
  114.5 31.4 %attn_fwd.1 = (bf16[4096,128]{1,0:T(8,128)(2,1)}, f32[16,512]{1,0:T(8,128)S(1)}) custom-call(s32[16,512]{1,0:T(8,128)S(1)} %get-tuple-element.32.lo_ref.start_ref, s32[16,512]{1,0:T(8,128)S(1)} %get-tuple-element.32.lo_ref.start_ref, bf16[4096,128]{1,0:T(8,128)(2,1)S(1)} %get-tuple-element.33.q_ref, bf16[4096,128]{1,0:T(8,128)(2,1)S(1)} %get-tuple-element.34.k_ref, ...), custom_call_target="tpu_custom_call" | custom-call | flops 20000000000 | bytes 5000000 | tf_op jit(solution)/shard_map/attn_fwd/pallas_call | solution.py:142
  145.9 2.3 all-to-all-start
  149.0 17.4 %all-to-all-done = bf16[8,512,128]{2,1,0:T(8,128)(2,1)S(1)} async-done(((bf16[8,512,128]{2,1,0:T(8,128)(2,1)}), bf16[8,512,128]{2,1,0:T(8,128)(2,1)S(1)}, u32[]{:S(2)}, u32[]{:S(2)}) %all-to-all-start) | async-done | bytes 1048608 | tf_op jit(solution)/shard_map/all_to_all | solution.py:718
  166.4 1.0 copy-done.8
  167.3 3.3 fusion.9
  170.7 1.3 fusion.3.z_ref
  172.0 35.7 %mlp_stage.1 = (bf16[512,1024]{1,0:T(8,128)(2,1)}, bf16[2816,512]{1,0:T(8,128)(2,1)}, f32[512,5632]{1,0:T(8,128)}) custom-call(bf16[512,1024]{1,0:T(8,128)(2,1)} %fusion.3.z_ref, bf16[512,1024]{1,0:T(8,128)(2,1)} %gy_ref.3, bf16[2816,1024]{1,0:T(8,128)(2,1)} %all-gather.4.cloned.1.call-done.wd_hbm, bf16[4,128,5632]{2,1,0:T(8,128)(2,1)} %bitcast.82), custom_call_target="tpu_custom_call" | custom-call | flops 20999999488 | bytes 40000000 | tf_op jit(solution)/shard_map/mlp_stage/pallas_call | solution.py:679
  207.7 1.2 copy-done.10
  209.5 0.7 fusion.8.gh_ref
  210.2 0.9 copy-done.25
  211.1 1.3 fusion.12
  212.4 1.2 copy.27
  213.5 2.5 all-to-all-start.1
  216.1 1.3 copy.23
  217.4 8.3 %fusion.10 = bf16[512,1024]{1,0:T(8,128)(2,1)} fusion(bf16[512,1024]{1,0:T(8,128)(2,1)} %copy-done.7, bf16[2816,512]{1,0:T(8,128)(2,1)} %get-tuple-element.39.mt_ref, bf16[2816,1024]{1,0:T(8,128)(2,1)} %all-gather.4.cloned.1.call-done.wd_hbm), kind=kOutput, calls=%fused_computation.13 | convolution fusion | flops 2954362880 | bytes 10747904 | tf_op jit(solution)/shard_map/dot_general | solution.py:31
  225.7 17.1 %all-to-all-done.1 = bf16[8,512,128]{2,1,0:T(8,128)(2,1)S(1)} async-done(((bf16[8,512,128]{2,1,0:T(8,128)(2,1)}), bf16[8,512,128]{2,1,0:T(8,128)(2,1)S(1)}, u32[]{:S(2)}, u32[]{:S(2)}) %all-to-all-start.1) | async-done | bytes 1048608 | tf_op jit(solution)/shard_map/all_to_all | solution.py:718
  242.8 1.2 copy-done.6
  244.0 47.7 %attn_bwd.1 = bf16[4096,384]{1,0:T(8,128)(2,1)} custom-call(s32[16,512]{1,0:T(8,128)S(1)} %get-tuple-element.32.lo_ref.start_ref, s32[16,512]{1,0:T(8,128)S(1)} %get-tuple-element.32.lo_ref.start_ref, f32[16,512]{1,0:T(8,128)S(1)} %get-tuple-element.41.lse_ref, bf16[4096,128]{1,0:T(8,128)(2,1)S(1)} %get-tuple-element.33.q_ref, ...), custom_call_target="tpu_custom_call" | custom-call | flops 49999998976 | bytes 12000000 | tf_op jit(solution)/shard_map/attn_bwd/pallas_call | solution.py:155
  291.7 150.2 %tail_stage.1 = (f32[352,1024]{1,0:T(8,128)}, f32[128,1024]{1,0:T(8,128)}, f32[8,128,128]{2,1,0:T(8,128)}, f32[8,128,128]{2,1,0:T(8,128)}, f32[8,128,128]{2,1,0:...) custom-call(bf16[2816,512]{1,0:T(8,128)(2,1)} %get-tuple-element.39.mt_ref, bf16[512,1024]{1,0:T(8,128)(2,1)} %gy_ref.3, ...), custom_call_target="tpu_custom_call" | custom-call | flops 60000002048 | bytes 60000000 | tf_op jit(solution)/shard_map/tail_stage/pallas_call | solution.py:534
  441.8 1.3 slice_bitcast_fusion.1
  443.1 3.6 fusion.14
  446.8 1.0 copy.34
  448.1 0.8 copy.35
  448.9 0.8 copy.36
  449.7 0.8 copy.37
  450.5 0.8 copy.38
  451.3 1.1 copy.39
  (69 shorter events, 2.2 us)
Async XLA Ops:
  7.2 3.5 copy-start.21
  7.2 3.5 copy-start.20
  7.2 3.5 copy-start.19
  7.2 164.7 %all-gather.6.cloned.1.call-start = ((), (), s32[]{:S(2)}) async-start(), calls=%async_computation.4 | async-start | bytes 7208960 | tf_op jit(solution)/shard_map/all_gather | solution.py:714
  9.8 1.9 copy-start.22
  9.8 1.9 copy-start.23
  9.8 1.9 copy-start.24
  9.8 2.2 copy-start.1
  9.8 2.1 copy-start.2
  9.9 162.1 %all-gather.4.cloned.1.call-start = ((), (), s32[]{:S(2)}) async-start(), calls=%async_computation.3 | async-start | bytes 6488064 | tf_op jit(solution)/shard_map/all_gather | solution.py:709
  10.6 281.0 %all-gather.8.cloned.1.call-start = ((), (), s32[]{:S(2)}) async-start(), calls=%async_computation.5 | async-start | bytes 3932160 | tf_op jit(solution)/shard_map/all_gather | solution.py:714
  12.0 1.1 copy-start
  114.5 31.4 %copy-start.3 = (bf16[4096,128]{1,0:T(8,128)(2,1)}, bf16[4096,128]{1,0:T(8,128)(2,1)S(1)}, u32[]{:S(2)}) copy-start(bf16[4096,128]{1,0:T(8,128)(2,1)S(1)} %get-tuple-element.34.k_ref) | copy-start | bytes 3145732
  114.5 31.4 %copy-start.5 = (bf16[4096,128]{1,0:T(8,128)(2,1)}, bf16[4096,128]{1,0:T(8,128)(2,1)S(1)}, u32[]{:S(2)}) copy-start(bf16[4096,128]{1,0:T(8,128)(2,1)S(1)} %get-tuple-element.35.v_ref) | copy-start | bytes 3145732
  145.9 20.5 %all-to-all-start = ((bf16[8,512,128]{2,1,0:T(8,128)(2,1)}), bf16[8,512,128]{2,1,0:T(8,128)(2,1)S(1)}, u32[]{:S(2)}, u32[]{:S(2)}) async-start(bf16[8,512,128]{2,1,0:T(8,128)(2,1)} %bitcast.10), calls=%async_computation | async-start | bytes 2097152 | tf_op jit(solution)/shard_map/all_to_all | solution.py:718
  148.2 295.0 %reduce-scatter.2.cloned.1.call-start = ((), (), s32[]{:S(2)}) async-start(), calls=%async_computation.6 | async-start | bytes 14417920 | tf_op jit(solution)/shard_map/reduce_scatter | solution.py:748
  166.4 1.0 copy-start.8
  170.6 38.8 %copy-start.7 = (bf16[512,1024]{1,0:T(8,128)(2,1)}, bf16[512,1024]{1,0:T(8,128)(2,1)S(1)}, u32[]{:S(2)}) copy-start(bf16[512,1024]{1,0:T(8,128)(2,1)S(1)} %get-tuple-element.60.h_ref) | copy-start | bytes 3145732
  207.7 1.2 copy-start.10
  207.7 1.7 copy-start.13
  209.5 1.6 copy-start.25
  210.2 2.2 copy-start.14
  212.4 3.7 copy-start.9
  213.5 29.2 %all-to-all-start.1 = ((bf16[8,512,128]{2,1,0:T(8,128)(2,1)}), bf16[8,512,128]{2,1,0:T(8,128)(2,1)S(1)}, u32[]{:S(2)}, u32[]{:S(2)}) async-start(bf16[8,512,128]{2,1,0:T(8,128)(2,1)} %bitcast.70), calls=%async_computation.1 | async-start | bytes 2097152 | tf_op jit(solution)/shard_map/all_to_all | solution.py:718
  217.4 25.4 %copy-start.4 = (bf16[4096,128]{1,0:T(8,128)(2,1)S(1)}, bf16[4096,128]{1,0:T(8,128)(2,1)}, u32[]{:S(2)}) copy-start(bf16[4096,128]{1,0:T(8,128)(2,1)} %copy-done.3) | copy-start | bytes 3145732
  242.8 1.2 copy-start.6
  443.1 3.7 copy-start.12
  446.8 1.3 copy-start.18
  446.8 2.1 copy-start.17
  446.8 2.9 copy-start.16
  448.1 2.4 copy-start.15
  448.1 3.2 copy-start.11
Sparse Core Ops, SparseCore 0:
  10.4 106.0 all-gather.5
  118.3 40.6 all-gather.3
  160.7 43.9 all-gather.7
  207.8 158.7 reduce-scatter.1

commit v3 on v2

--- a/solution.py
+++ b/solution.py
@@ -344,7 +344,7 @@
 
 
 def tail_kernel(mt_ref, gy_ref, ot_ref, gh_ref, d_ref, x_ref, h_ref, gz_ref, gain_ref, u_hbm, win_hbm,
-                dn_out, wo_out, gq_out, gk_out, gv_out, gx_out, gain_out,
+                dn_out, wo_out, gq_out, gk_out, gv_out, gx_out, gain1_out, gain2_out,
                 mt_mate, gy_mate, ot_mate, gh_mate, part, box, d_buf, win_buf, u_buf, gw_acc, gw_in, gain_mine, gain_buf,
                 mate_send, mate_recv, rs_send, rs_recv, d_send, d_recv, gw_send, gw_recv, gg_send, gg_recv, win_send, win_recv, win_sem, u_sem):
     me = lax.axis_index('sp')
@@ -509,7 +509,8 @@
     total = gain_buf[0]
     for n in range(1, NDEV):
         total = total + gain_buf[n]
-    gain_out[...] = total
+    gain1_out[...] = total[0:1]
+    gain2_out[...] = total[1:2]
     for col in range(2):
         moves[4 + col].wait_recv()
 
@@ -535,9 +536,9 @@
         tail_kernel,
         out_shape=(jax.ShapeDtypeStruct((DN_ROWS, D), F32), jax.ShapeDtypeStruct((LANES, D), F32),
                    *(jax.ShapeDtypeStruct((NDEV, LANES, LANES), F32),) * 3, jax.ShapeDtypeStruct((TOK, D), BF16),
-                   jax.ShapeDtypeStruct((8, LANES), F32)),
+                   *(jax.ShapeDtypeStruct((1, LANES), F32),) * 2),
         in_specs=[VMEM_SPEC] * 9 + [pl.BlockSpec(memory_space=pltpu.HBM)] * 2,
-        out_specs=(VMEM_SPEC,) * 7,
+        out_specs=(VMEM_SPEC,) * 8,
         scratch_shapes=[pltpu.VMEM((4, DN_ROWS, TOK), BF16), pltpu.VMEM((TOK, D), BF16),
                         pltpu.VMEM((4, LANES, TOK), BF16), pltpu.VMEM((TOK, D), BF16),
                         pltpu.VMEM((4, 2, OUT_ROWS, COLS), F32), pltpu.VMEM((6, OUT_ROWS, COLS), F32),
@@ -695,6 +696,39 @@
     )(z, grad_y, wd_full, w_half)
 
 
+def emit_kernel(*refs):
+    count = (len(refs) - 1) // 3
+    sources, targets, bufs = refs[:count - 1], refs[count - 1:2 * count - 1], refs[2 * count - 1:3 * count - 1]
+    load_sem, store_sem = refs[-2:]
+    gu = sources[0]
+    views = [gu.at[:, 0:FF], gu.at[:, FF:2 * FF]] + list(sources[1:])
+    loads = [pltpu.make_async_copy(v, b, load_sem.at[n]) for n, (v, b) in enumerate(zip(views, bufs))]
+    stores = [pltpu.make_async_copy(b, t, store_sem.at[n]) for n, (b, t) in enumerate(zip(bufs, targets))]
+    order = list(range(2, count)) + [0, 1]
+    for n in order:
+        loads[n].start()
+    for n in order:
+        loads[n].wait()
+        stores[n].start()
+    for n in order:
+        stores[n].wait()
+
+
+def emit(grad_gu, *rest):
+    shapes = [jax.ShapeDtypeStruct((LANES, FF), F32)] * 2 + [jax.ShapeDtypeStruct(t.shape, t.dtype) for t in rest]
+    dma = pltpu.SemaphoreType.DMA
+    return pl.pallas_call(
+        emit_kernel,
+        out_shape=tuple(shapes),
+        in_specs=[pl.BlockSpec(memory_space=pl.ANY)] * (1 + len(rest)),
+        out_specs=(pl.BlockSpec(memory_space=pl.ANY),) * len(shapes),
+        scratch_shapes=[pltpu.VMEM(t.shape, t.dtype) for t in shapes] + [dma((len(shapes),)), dma((len(shapes),))],
+        compiler_params=pltpu.CompilerParams(vmem_limit_bytes=60 * 1024 * 1024),
+        cost_estimate=pl.CostEstimate(flops=1_000_000, bytes_accessed=15_000_000, transcendentals=0),
+        name='emit',
+    )(grad_gu, *rest)
+
+
 def rms_back(grad_out, normed, inv_rms):
     mean_term = jnp.mean(grad_out * normed, axis=-1, keepdims=True)
     return inv_rms * (grad_out - normed * mean_term)
@@ -753,12 +787,14 @@
         y = (h_wide + dot_tn(m_t, wd_full)).astype(BF16)
 
         d_qkv = attn_backward(start2, lse, q, k, v, o_own, grad_o, cos_t, sin_t)
-        grad_wdown, grad_wo, *grad_qkv, grad_x, grad_gains = tail_stage(
+        grad_wdown, grad_wo, *grad_qkv, grad_x, grad_gain1, grad_gain2 = tail_stage(
             m_t, grad_y, o_t, grad_h, d_qkv.reshape(NDEV, TOK, 3 * LANES), x, h_res, grad_z_b,
             gain1, u_all, win_half)
+        grad_wgate, grad_wup, grad_wdown, grad_wo, *grad_qkv, grad_x, grad_gain1, grad_gain2 = emit(
+            grad_wgu, grad_wdown, grad_wo, *grad_qkv, grad_x, grad_gain1, grad_gain2)
         grad_q, grad_k, grad_v = (t.reshape(16, HD, LANES).transpose(2, 0, 1) for t in grad_qkv)
-        return (y, grad_x, grad_gains[0], grad_q, grad_k, grad_v, grad_wo.reshape(2, HD, D),
-                grad_gains[1], grad_wgu[:, :FF], grad_wgu[:, FF:], grad_wdown)
+        return (y, grad_x, grad_gain1.reshape(LANES), grad_q, grad_k, grad_v, grad_wo.reshape(2, HD, D),
+                grad_gain2.reshape(LANES), grad_wgate, grad_wup, grad_wdown)
 
     return jax.shard_map(
         local_layer, mesh=mesh,

time: 459 us -> 455 us (level)
  local copies, waits for them, and re-layouts: 19.2 us -> 8.66 us
  Pallas kernels: 366 us -> 373 us
    pallas_call x0 -> x1, Pallas kernels: none -> 6.21 us  [emit(): pl.pallas_call(emit_kernel, out_shape=tuple(shapes), in_specs=[pl.BlockSp...]
    unnamed x58 -> x40, local copies, waits for them, and re-layouts: 11 us -> 5.44 us
  transfers between devices with their start and end apart: 6 -> 6, of which waited for: 2 -> 2; matrix products, arithmetic and copies ran while one was open for 5% -> 4% of each run, Pallas kernels for 80% -> 81%
where the time goes in v3:
time: 455 us
  Pallas kernels  373 us (82%)
  waiting for transfers between devices  35.2 us (8%)
  between operations  14.1 us (3%)
  matrix products  12.9 us (3%)
  local copies, waits for them, and re-layouts  8.66 us (2%)
  other arithmetic  6.18 us (1%)
  starting transfers between devices  5.14 us (1%)
    pallas_call x1, Pallas kernels, tail_stage(): pl.pallas_call(tail_kernel, out_shape=(jax.ShapeDtypeStruct((DN_ROWS, D),...  150 us
    pallas_call x1, Pallas kernels, head_stage(): pl.pallas_call(head_kernel, out_shape=(jax.ShapeDtypeStruct((SEQ, D), BF1...  101 us
    pallas_call x1, Pallas kernels, attn_backward(): pl.pallas_call(attn_bwd_kernel, out_shape=jax.ShapeDtypeStruct((SEQ, 3 *...  47.7 us
    pallas_call x1, Pallas kernels, mlp_stage(): pl.pallas_call(mlp_kernel, out_shape=(jax.ShapeDtypeStruct((TOK, D), BF16...  35.7 us
    all_to_all x2, waiting for transfers between devices, exchange(): return lax.all_to_all(t, 'sp', 0, 0)  34.4 us
    pallas_call x1, Pallas kernels, attn_forward(): pl.pallas_call(attn_fwd_kernel, out_shape=(jax.ShapeDtypeStruct((SEQ, LAN...  31.4 us
  transfers between devices with their start and end apart: 6, of which 2 were waited for; matrix products, arithmetic and copies ran while one was open for 4% of the time, Pallas kernels for 81%

profile of v3, /device:TPU:0, one launch (start us, length us, event | category | flops | bytes accessed | tf_op | source)
XLA Modules:
  0.0 454.7 jit_solution(10694440352968717936)
XLA Ops:
  7.3 2.6 pad_maximum_fusion
  9.9 0.0 all-gather.4.cloned.1.call-start
  9.9 0.7 all-gather.4.cloned.1.call-update
  10.7 1.0 pad_maximum_fusion.1.w_ref
  11.8 0.1 pad.5.clone
  11.8 0.1 maximum_maximum_fusion.small_ref
  11.9 0.1 broadcast_in_dim.28.freq_ref
  12.0 1.1 copy-done
  13.1 101.4 %head_stage.1 = (bf16[4096,1024]{1,0:T(8,128)(2,1)}, bf16[4096,128]{1,0:T(8,128)(2,1)S(1)}, bf16[4096,128]{1,0:T(8,128)(2,1)S(1)}, bf16[4096,128]{1,0:T(8,128)(2...) custom-call(bf16[512,1024]{1,0:T(8,128)(2,1)S(1)} %copy-done.1, ...), custom_call_target="tpu_custom_call" | custom-call | flops 40000000000 | bytes 30000000 | tf_op jit(solution)/shard_map/head_stage/pallas_call | solution.py:322
  114.5 31.4 %attn_fwd.1 = (bf16[4096,128]{1,0:T(8,128)(2,1)}, f32[16,512]{1,0:T(8,128)S(1)}) custom-call(s32[16,512]{1,0:T(8,128)S(1)} %get-tuple-element.43.lo_ref.start_ref, s32[16,512]{1,0:T(8,128)S(1)} %get-tuple-element.43.lo_ref.start_ref, bf16[4096,128]{1,0:T(8,128)(2,1)S(1)} %get-tuple-element.44.q_ref, bf16[4096,128]{1,0:T(8,128)(2,1)S(1)} %get-tuple-element.45.k_ref, ...), custom_call_target="tpu_custom_call" | custom-call | flops 20000000000 | bytes 5000000 | tf_op jit(solution)/shard_map/attn_fwd/pallas_call | solution.py:142
  145.9 2.3 all-to-all-start
  148.2 0.2 reduce-scatter.2.cloned.1.call-start
  148.4 0.6 slice_bitcast_fusion
  149.0 17.4 %all-to-all-done = bf16[8,512,128]{2,1,0:T(8,128)(2,1)S(1)} async-done(((bf16[8,512,128]{2,1,0:T(8,128)(2,1)}), bf16[8,512,128]{2,1,0:T(8,128)(2,1)S(1)}, u32[]{:S(2)}, u32[]{:S(2)}) %all-to-all-start) | async-done | bytes 1048608 | tf_op jit(solution)/shard_map/all_to_all | solution.py:752
  166.4 1.0 copy-done.8
  167.4 3.3 fusion.9
  170.7 1.3 fusion.3.z_ref
  172.0 35.7 %mlp_stage.1 = (bf16[512,1024]{1,0:T(8,128)(2,1)}, bf16[2816,512]{1,0:T(8,128)(2,1)}, f32[512,5632]{1,0:T(8,128)}) custom-call(bf16[512,1024]{1,0:T(8,128)(2,1)} %fusion.3.z_ref, bf16[512,1024]{1,0:T(8,128)(2,1)} %gy_ref.3, bf16[2816,1024]{1,0:T(8,128)(2,1)} %all-gather.4.cloned.1.call-done.wd_hbm, bf16[4,128,5632]{2,1,0:T(8,128)(2,1)} %bitcast.76), custom_call_target="tpu_custom_call" | custom-call | flops 20999999488 | bytes 40000000 | tf_op jit(solution)/shard_map/mlp_stage/pallas_call | solution.py:680
  207.8 1.2 copy-done.10
  209.0 0.5 fusion.4
  209.5 0.7 fusion.8.gh_ref
  210.3 0.9 copy-done.19
  211.1 1.3 fusion.12
  212.4 1.2 copy.27
  213.6 2.5 all-to-all-start.1
  216.1 1.3 copy.23
  217.4 8.3 %fusion.10 = bf16[512,1024]{1,0:T(8,128)(2,1)} fusion(bf16[512,1024]{1,0:T(8,128)(2,1)} %copy-done.7, bf16[2816,512]{1,0:T(8,128)(2,1)} %get-tuple-element.50.mt_ref, bf16[2816,1024]{1,0:T(8,128)(2,1)} %all-gather.4.cloned.1.call-done.wd_hbm), kind=kOutput, calls=%fused_computation.13 | convolution fusion | flops 2954362880 | bytes 10747904 | tf_op jit(solution)/shard_map/dot_general | solution.py:31
  225.8 17.1 %all-to-all-done.1 = bf16[8,512,128]{2,1,0:T(8,128)(2,1)S(1)} async-done(((bf16[8,512,128]{2,1,0:T(8,128)(2,1)}), bf16[8,512,128]{2,1,0:T(8,128)(2,1)S(1)}, u32[]{:S(2)}, u32[]{:S(2)}) %all-to-all-start.1) | async-done | bytes 1048608 | tf_op jit(solution)/shard_map/all_to_all | solution.py:752
  242.8 1.2 copy-done.6
  244.0 47.7 %attn_bwd.1 = bf16[4096,384]{1,0:T(8,128)(2,1)} custom-call(s32[16,512]{1,0:T(8,128)S(1)} %get-tuple-element.43.lo_ref.start_ref, s32[16,512]{1,0:T(8,128)S(1)} %get-tuple-element.43.lo_ref.start_ref, f32[16,512]{1,0:T(8,128)S(1)} %get-tuple-element.53.lse_ref, bf16[4096,128]{1,0:T(8,128)(2,1)S(1)} %get-tuple-element.44.q_ref, ...), custom_call_target="tpu_custom_call" | custom-call | flops 49999998976 | bytes 12000000 | tf_op jit(solution)/shard_map/attn_bwd/pallas_call | solution.py:155
  291.7 150.2 %tail_stage.1 = (f32[352,1024]{1,0:T(8,128)}, f32[128,1024]{1,0:T(8,128)}, f32[8,128,128]{2,1,0:T(8,128)}, f32[8,128,128]{2,1,0:T(8,128)}, f32[8,128,128]{2,1,0:...) custom-call(bf16[2816,512]{1,0:T(8,128)(2,1)} %get-tuple-element.50.mt_ref, ...), custom_call_target="tpu_custom_call" | custom-call | flops 60000002048 | bytes 60000000 | tf_op jit(solution)/shard_map/tail_stage/pallas_call | solution.py:535
  441.9 6.2 %emit.1 = (f32[128,2816]{1,0:T(8,128)}, f32[128,2816]{1,0:T(8,128)}, f32[352,1024]{1,0:T(8,128)}, f32[128,1024]{1,0:T(8,128)}, f32[8,128,128]{2,1,0:T(8,128)}, /...) custom-call(f32[128,5632]{1,0:T(8,128)} %reduce-scatter.2.cloned.1.c, ...), custom_call_target="tpu_custom_call" | custom-call | flops 1000000 | bytes 15000000 | tf_op jit(solution)/shard_map/emit/pallas_call | solution.py:720
  (50 shorter events, 0.3 us)
Async XLA Ops:
  7.2 3.5 copy-start.15
  7.2 3.5 copy-start.14
  7.2 3.5 copy-start.13
  7.2 164.8 %all-gather.6.cloned.1.call-start = ((), (), s32[]{:S(2)}) async-start(), calls=%async_computation.4 | async-start | bytes 7208960 | tf_op jit(solution)/shard_map/all_gather | solution.py:748
  9.8 1.9 copy-start.16
  9.8 1.9 copy-start.17
  9.8 1.9 copy-start.18
  9.8 2.1 copy-start.1
  9.8 2.1 copy-start.2
  9.9 162.1 %all-gather.4.cloned.1.call-start = ((), (), s32[]{:S(2)}) async-start(), calls=%async_computation.3 | async-start | bytes 6488064 | tf_op jit(solution)/shard_map/all_gather | solution.py:743
  10.6 281.1 %all-gather.8.cloned.1.call-start = ((), (), s32[]{:S(2)}) async-start(), calls=%async_computation.6 | async-start | bytes 3932160 | tf_op jit(solution)/shard_map/all_gather | solution.py:748
  12.0 1.1 copy-start
  114.5 31.4 %copy-start.3 = (bf16[4096,128]{1,0:T(8,128)(2,1)}, bf16[4096,128]{1,0:T(8,128)(2,1)S(1)}, u32[]{:S(2)}) copy-start(bf16[4096,128]{1,0:T(8,128)(2,1)S(1)} %get-tuple-element.45.k_ref) | copy-start | bytes 3145732
  114.5 31.4 %copy-start.5 = (bf16[4096,128]{1,0:T(8,128)(2,1)}, bf16[4096,128]{1,0:T(8,128)(2,1)S(1)}, u32[]{:S(2)}) copy-start(bf16[4096,128]{1,0:T(8,128)(2,1)S(1)} %get-tuple-element.46.v_ref) | copy-start | bytes 3145732
  145.9 20.5 %all-to-all-start = ((bf16[8,512,128]{2,1,0:T(8,128)(2,1)}), bf16[8,512,128]{2,1,0:T(8,128)(2,1)S(1)}, u32[]{:S(2)}, u32[]{:S(2)}) async-start(bf16[8,512,128]{2,1,0:T(8,128)(2,1)} %bitcast.10), calls=%async_computation | async-start | bytes 2097152 | tf_op jit(solution)/shard_map/all_to_all | solution.py:752
  148.2 293.7 %reduce-scatter.2.cloned.1.call-start = ((), (), s32[]{:S(2)}) async-start(), calls=%async_computation.5 | async-start | bytes 14417920 | tf_op jit(solution)/shard_map/reduce_scatter | solution.py:782
  166.4 1.0 copy-start.8
  170.7 38.8 %copy-start.7 = (bf16[512,1024]{1,0:T(8,128)(2,1)}, bf16[512,1024]{1,0:T(8,128)(2,1)S(1)}, u32[]{:S(2)}) copy-start(bf16[512,1024]{1,0:T(8,128)(2,1)S(1)} %get-tuple-element.78.h_ref) | copy-start | bytes 3145732
  207.7 1.2 copy-start.10
  207.8 1.7 copy-start.11
  209.5 1.6 copy-start.19
  210.2 2.2 copy-start.12
  212.4 3.7 copy-start.9
  213.6 29.2 %all-to-all-start.1 = ((bf16[8,512,128]{2,1,0:T(8,128)(2,1)}), bf16[8,512,128]{2,1,0:T(8,128)(2,1)S(1)}, u32[]{:S(2)}, u32[]{:S(2)}) async-start(bf16[8,512,128]{2,1,0:T(8,128)(2,1)} %bitcast.68), calls=%async_computation.2 | async-start | bytes 2097152 | tf_op jit(solution)/shard_map/all_to_all | solution.py:752
  217.4 25.4 %copy-start.4 = (bf16[4096,128]{1,0:T(8,128)(2,1)S(1)}, bf16[4096,128]{1,0:T(8,128)(2,1)}, u32[]{:S(2)}) copy-start(bf16[4096,128]{1,0:T(8,128)(2,1)} %copy-done.3) | copy-start | bytes 3145732
  242.8 1.2 copy-start.6
Sparse Core Ops, SparseCore 0:
  10.4 106.0 all-gather.5
  118.3 40.6 all-gather.3
  160.7 43.9 all-gather.7
  207.9 158.6 reduce-scatter.1

commit v4 on v3

--- a/solution.py
+++ b/solution.py
@@ -17,6 +17,7 @@
 LANES = 128
 BQ = 256
 BK = 512
+BK_BWD = 256
 NQ = SEQ // BQ
 NEG = -1e30
 F32 = jnp.float32
@@ -101,21 +102,21 @@
         dq_acc[...] = jnp.zeros_like(dq_acc)
 
         def k_block(j, _):
-            k_start = pl.multiple_of(j * BK, BK)
-            k = k_ref[pl.ds(k_start, BK), :]
-            v = v_ref[pl.ds(k_start, BK), :]
+            k_start = pl.multiple_of(j * BK_BWD, BK_BWD)
+            k = k_ref[pl.ds(k_start, BK_BWD), :]
+            v = v_ref[pl.ds(k_start, BK_BWD), :]
             s = dot_nt(k, q2)
             k_index = k_start + lax.broadcasted_iota(jnp.int32, s.shape, 0)
             s = jnp.where((k_index >= first) & (k_index <= q_index), s, NEG)
             p = jnp.exp(s - lse)
             dp = dot_nt(v, do2).astype(BF16).astype(F32)
             ds = (p * (dp - delta)).astype(BF16)
-            dv_acc[pl.ds(k_start, BK), :] += jnp.dot(p.astype(BF16), do2, preferred_element_type=F32)
-            dk_acc[pl.ds(k_start, BK), :] += jnp.dot(ds, q2, preferred_element_type=F32)
+            dv_acc[pl.ds(k_start, BK_BWD), :] += jnp.dot(p.astype(BF16), do2, preferred_element_type=F32)
+            dk_acc[pl.ds(k_start, BK_BWD), :] += jnp.dot(ds, q2, preferred_element_type=F32)
             dq_acc[...] += dot_tn(k, ds)
             return 0
 
-        lax.fori_loop(lax.div(lo_ref[i, 0], BK), (q_start + BQ - 1) // BK + 1, k_block, 0)
+        lax.fori_loop(lax.div(lo_ref[i, 0], BK_BWD), (q_start + BQ - 1) // BK_BWD + 1, k_block, 0)
         dq = jnp.concatenate([dq_acc[:HD, :BQ], dq_acc[HD:, BQ:]], axis=0).T * (HD ** -0.5)
         rows = pl.ds(q_start, BQ)
         dq = dq.astype(BF16).astype(F32)

time: 455 us -> 455 us (level)
  no operation moved by 1% of the time
where the time goes in v4:
time: 455 us
  Pallas kernels  373 us (82%)
  waiting for transfers between devices  35.2 us (8%)
  between operations  14.1 us (3%)
  matrix products  12.9 us (3%)
  local copies, waits for them, and re-layouts  8.66 us (2%)
  other arithmetic  6.18 us (1%)
  starting transfers between devices  5.14 us (1%)
    pallas_call x1, Pallas kernels, tail_stage(): pl.pallas_call(tail_kernel, out_shape=(jax.ShapeDtypeStruct((DN_ROWS, D),...  153 us
    pallas_call x1, Pallas kernels, head_stage(): pl.pallas_call(head_kernel, out_shape=(jax.ShapeDtypeStruct((SEQ, D), BF1...  101 us
    pallas_call x1, Pallas kernels, attn_backward(): pl.pallas_call(attn_bwd_kernel, out_shape=jax.ShapeDtypeStruct((SEQ, 3 *...  45.2 us
    pallas_call x1, Pallas kernels, mlp_stage(): pl.pallas_call(mlp_kernel, out_shape=(jax.ShapeDtypeStruct((TOK, D), BF16...  35.7 us
    all_to_all x2, waiting for transfers between devices, exchange(): return lax.all_to_all(t, 'sp', 0, 0)  34.4 us
    pallas_call x1, Pallas kernels, attn_forward(): pl.pallas_call(attn_fwd_kernel, out_shape=(jax.ShapeDtypeStruct((SEQ, LAN...  31.4 us
  transfers between devices with their start and end apart: 6, of which 2 were waited for; matrix products, arithmetic and copies ran while one was open for 4% of the time, Pallas kernels for 81%

profile of v4, /device:TPU:0, one launch (start us, length us, event | category | flops | bytes accessed | tf_op | source)
XLA Modules:
  0.0 454.7 jit_solution(1089319535458372631)
XLA Ops:
  7.3 2.6 pad_maximum_fusion
  9.9 0.0 all-gather.4.cloned.1.call-start
  9.9 0.7 all-gather.4.cloned.1.call-update
  10.7 1.0 pad_maximum_fusion.1.w_ref
  11.8 0.1 pad.5.clone
  11.8 0.1 maximum_maximum_fusion.small_ref
  11.9 0.1 broadcast_in_dim.28.freq_ref
  12.0 1.1 copy-done
  13.1 101.4 %head_stage.1 = (bf16[4096,1024]{1,0:T(8,128)(2,1)}, bf16[4096,128]{1,0:T(8,128)(2,1)S(1)}, bf16[4096,128]{1,0:T(8,128)(2,1)S(1)}, bf16[4096,128]{1,0:T(8,128)(2...) custom-call(bf16[512,1024]{1,0:T(8,128)(2,1)S(1)} %copy-done.1, ...), custom_call_target="tpu_custom_call" | custom-call | flops 40000000000 | bytes 30000000 | tf_op jit(solution)/shard_map/head_stage/pallas_call | solution.py:323
  114.5 31.4 %attn_fwd.1 = (bf16[4096,128]{1,0:T(8,128)(2,1)}, f32[16,512]{1,0:T(8,128)S(1)}) custom-call(s32[16,512]{1,0:T(8,128)S(1)} %get-tuple-element.43.lo_ref.start_ref, s32[16,512]{1,0:T(8,128)S(1)} %get-tuple-element.43.lo_ref.start_ref, bf16[4096,128]{1,0:T(8,128)(2,1)S(1)} %get-tuple-element.44.q_ref, bf16[4096,128]{1,0:T(8,128)(2,1)S(1)} %get-tuple-element.45.k_ref, ...), custom_call_target="tpu_custom_call" | custom-call | flops 20000000000 | bytes 5000000 | tf_op jit(solution)/shard_map/attn_fwd/pallas_call | solution.py:143
  145.9 2.3 all-to-all-start
  148.2 0.2 reduce-scatter.2.cloned.1.call-start
  148.4 0.6 slice_bitcast_fusion
  149.0 17.4 %all-to-all-done = bf16[8,512,128]{2,1,0:T(8,128)(2,1)S(1)} async-done(((bf16[8,512,128]{2,1,0:T(8,128)(2,1)}), bf16[8,512,128]{2,1,0:T(8,128)(2,1)S(1)}, u32[]{:S(2)}, u32[]{:S(2)}) %all-to-all-start) | async-done | bytes 1048608 | tf_op jit(solution)/shard_map/all_to_all | solution.py:753
  166.4 1.0 copy-done.8
  167.4 3.3 fusion.9
  170.7 1.3 fusion.3.z_ref
  172.0 35.7 %mlp_stage.1 = (bf16[512,1024]{1,0:T(8,128)(2,1)}, bf16[2816,512]{1,0:T(8,128)(2,1)}, f32[512,5632]{1,0:T(8,128)}) custom-call(bf16[512,1024]{1,0:T(8,128)(2,1)} %fusion.3.z_ref, bf16[512,1024]{1,0:T(8,128)(2,1)} %gy_ref.3, bf16[2816,1024]{1,0:T(8,128)(2,1)} %all-gather.4.cloned.1.call-done.wd_hbm, bf16[4,128,5632]{2,1,0:T(8,128)(2,1)} %bitcast.76), custom_call_target="tpu_custom_call" | custom-call | flops 20999999488 | bytes 40000000 | tf_op jit(solution)/shard_map/mlp_stage/pallas_call | solution.py:681
  207.8 1.2 copy-done.10
  209.0 0.5 fusion.4
  209.5 0.7 fusion.8.gh_ref
  210.3 0.9 copy-done.19
  211.1 1.3 fusion.12
  212.4 1.2 copy.27
  213.6 2.5 all-to-all-start.1
  216.1 1.3 copy.23
  217.4 8.3 %fusion.10 = bf16[512,1024]{1,0:T(8,128)(2,1)} fusion(bf16[512,1024]{1,0:T(8,128)(2,1)} %copy-done.7, bf16[2816,512]{1,0:T(8,128)(2,1)} %get-tuple-element.50.mt_ref, bf16[2816,1024]{1,0:T(8,128)(2,1)} %all-gather.4.cloned.1.call-done.wd_hbm), kind=kOutput, calls=%fused_computation.13 | convolution fusion | flops 2954362880 | bytes 10747904 | tf_op jit(solution)/shard_map/dot_general | solution.py:32
  225.8 17.1 %all-to-all-done.1 = bf16[8,512,128]{2,1,0:T(8,128)(2,1)S(1)} async-done(((bf16[8,512,128]{2,1,0:T(8,128)(2,1)}), bf16[8,512,128]{2,1,0:T(8,128)(2,1)S(1)}, u32[]{:S(2)}, u32[]{:S(2)}) %all-to-all-start.1) | async-done | bytes 1048608 | tf_op jit(solution)/shard_map/all_to_all | solution.py:753
  242.8 1.2 copy-done.6
  244.0 45.2 %attn_bwd.1 = bf16[4096,384]{1,0:T(8,128)(2,1)} custom-call(s32[16,512]{1,0:T(8,128)S(1)} %get-tuple-element.43.lo_ref.start_ref, s32[16,512]{1,0:T(8,128)S(1)} %get-tuple-element.43.lo_ref.start_ref, f32[16,512]{1,0:T(8,128)S(1)} %get-tuple-element.53.lse_ref, bf16[4096,128]{1,0:T(8,128)(2,1)S(1)} %get-tuple-element.44.q_ref, ...), custom_call_target="tpu_custom_call" | custom-call | flops 49999998976 | bytes 12000000 | tf_op jit(solution)/shard_map/attn_bwd/pallas_call | solution.py:156
  289.2 152.7 %tail_stage.1 = (f32[352,1024]{1,0:T(8,128)}, f32[128,1024]{1,0:T(8,128)}, f32[8,128,128]{2,1,0:T(8,128)}, f32[8,128,128]{2,1,0:T(8,128)}, f32[8,128,128]{2,1,0:...) custom-call(bf16[2816,512]{1,0:T(8,128)(2,1)} %get-tuple-element.50.mt_ref, ...), custom_call_target="tpu_custom_call" | custom-call | flops 60000002048 | bytes 60000000 | tf_op jit(solution)/shard_map/tail_stage/pallas_call | solution.py:536
  441.9 6.2 %emit.1 = (f32[128,2816]{1,0:T(8,128)}, f32[128,2816]{1,0:T(8,128)}, f32[352,1024]{1,0:T(8,128)}, f32[128,1024]{1,0:T(8,128)}, f32[8,128,128]{2,1,0:T(8,128)}, /...) custom-call(f32[128,5632]{1,0:T(8,128)} %reduce-scatter.2.cloned.1.c, ...), custom_call_target="tpu_custom_call" | custom-call | flops 1000000 | bytes 15000000 | tf_op jit(solution)/shard_map/emit/pallas_call | solution.py:721
  (50 shorter events, 0.3 us)
Async XLA Ops:
  7.2 3.5 copy-start.15
  7.2 3.5 copy-start.14
  7.2 3.5 copy-start.13
  7.2 164.8 %all-gather.6.cloned.1.call-start = ((), (), s32[]{:S(2)}) async-start(), calls=%async_computation.4 | async-start | bytes 7208960 | tf_op jit(solution)/shard_map/all_gather | solution.py:749
  9.8 1.9 copy-start.16
  9.8 1.9 copy-start.17
  9.8 1.9 copy-start.18
  9.8 2.1 copy-start.1
  9.8 2.1 copy-start.2
  9.9 162.1 %all-gather.4.cloned.1.call-start = ((), (), s32[]{:S(2)}) async-start(), calls=%async_computation.3 | async-start | bytes 6488064 | tf_op jit(solution)/shard_map/all_gather | solution.py:744
  10.6 278.6 %all-gather.8.cloned.1.call-start = ((), (), s32[]{:S(2)}) async-start(), calls=%async_computation.6 | async-start | bytes 3932160 | tf_op jit(solution)/shard_map/all_gather | solution.py:749
  12.0 1.1 copy-start
  114.5 31.4 %copy-start.3 = (bf16[4096,128]{1,0:T(8,128)(2,1)}, bf16[4096,128]{1,0:T(8,128)(2,1)S(1)}, u32[]{:S(2)}) copy-start(bf16[4096,128]{1,0:T(8,128)(2,1)S(1)} %get-tuple-element.45.k_ref) | copy-start | bytes 3145732
  114.5 31.4 %copy-start.5 = (bf16[4096,128]{1,0:T(8,128)(2,1)}, bf16[4096,128]{1,0:T(8,128)(2,1)S(1)}, u32[]{:S(2)}) copy-start(bf16[4096,128]{1,0:T(8,128)(2,1)S(1)} %get-tuple-element.46.v_ref) | copy-start | bytes 3145732
  145.9 20.5 %all-to-all-start = ((bf16[8,512,128]{2,1,0:T(8,128)(2,1)}), bf16[8,512,128]{2,1,0:T(8,128)(2,1)S(1)}, u32[]{:S(2)}, u32[]{:S(2)}) async-start(bf16[8,512,128]{2,1,0:T(8,128)(2,1)} %bitcast.10), calls=%async_computation | async-start | bytes 2097152 | tf_op jit(solution)/shard_map/all_to_all | solution.py:753
  148.2 293.7 %reduce-scatter.2.cloned.1.call-start = ((), (), s32[]{:S(2)}) async-start(), calls=%async_computation.5 | async-start | bytes 14417920 | tf_op jit(solution)/shard_map/reduce_scatter | solution.py:783
  166.4 1.0 copy-start.8
  170.7 38.8 %copy-start.7 = (bf16[512,1024]{1,0:T(8,128)(2,1)}, bf16[512,1024]{1,0:T(8,128)(2,1)S(1)}, u32[]{:S(2)}) copy-start(bf16[512,1024]{1,0:T(8,128)(2,1)S(1)} %get-tuple-element.78.h_ref) | copy-start | bytes 3145732
  207.7 1.2 copy-start.10
  207.8 1.7 copy-start.11
  209.5 1.6 copy-start.19
  210.2 2.2 copy-start.12
  212.4 3.7 copy-start.9
  213.6 29.2 %all-to-all-start.1 = ((bf16[8,512,128]{2,1,0:T(8,128)(2,1)}), bf16[8,512,128]{2,1,0:T(8,128)(2,1)S(1)}, u32[]{:S(2)}, u32[]{:S(2)}) async-start(bf16[8,512,128]{2,1,0:T(8,128)(2,1)} %bitcast.68), calls=%async_computation.2 | async-start | bytes 2097152 | tf_op jit(solution)/shard_map/all_to_all | solution.py:753
  217.4 25.4 %copy-start.4 = (bf16[4096,128]{1,0:T(8,128)(2,1)S(1)}, bf16[4096,128]{1,0:T(8,128)(2,1)}, u32[]{:S(2)}) copy-start(bf16[4096,128]{1,0:T(8,128)(2,1)} %copy-done.3) | copy-start | bytes 3145732
  242.8 1.2 copy-start.6
Sparse Core Ops, SparseCore 0:
  10.4 106.0 all-gather.5
  118.3 40.6 all-gather.3
  160.7 43.9 all-gather.7
  207.9 160.2 reduce-scatter.1
